TPU v7x, 8 devices: a whole 2x2x1 slice. The times are simulated.
8 devices in a mesh: col: 4 (over z, y, x), row: 2 (over core).
Axes of the slice: x: 2, y: 2, z: 1, core: 2. Of those that a mesh axis runs over, the one named last changes fastest.
Arguments:
- t_amps: float32 [256, 9216], P('row', 'col')
- denoms: float32 [256, 9216], P('row', 'col')
- v_oovv: bfloat16 [256, 9216], P('row', 'col')
- v_vvvv: bfloat16 [9216, 9216], P('row', 'col')
- v_oooo: bfloat16 [256, 256], replicated
- w_direct: bfloat16 [1536, 1536], P(None, 'col')
- w_exch: bfloat16 [1536, 1536], P(None, 'col')
Outputs:
- output: float32 [256, 9216], P('row', 'col')
All inputs are finite; a program needn't handle non-finite values.
Results may differ from a plain program's by a relative error of at most 0.001.
Values are sent between devices in bfloat16 or wider.
A program may use at most 1 GiB of HBM per device.

v0:
```python
import math
import jax
import jax.numpy as jnp
from jax import lax
from jax.sharding import PartitionSpec as P


def solution(mesh):
    n_row = mesh.shape["row"]
    n_col = mesh.shape["col"]
    amp_spec = P("row", "col")
    wide_spec = P(None, "col")

    def local_sweep(t_blk, d_blk, oovv_blk, vvvv_blk, oooo_full, wd_blk, wx_blk):
        rows_dev, cols_dev = t_blk.shape
        n_occ = math.isqrt(oooo_full.shape[0])
        n_virt = wd_blk.shape[0] // n_occ
        occ_row = n_occ // n_row
        occ_col = n_occ // n_col
        t_half = t_blk.astype(jnp.bfloat16)
        t_rows = lax.all_gather(t_half, "col", axis=1, tiled=True)
        t_ladder = lax.all_to_all(t_rows, "row", 1, 0, tiled=True)
        ladder_part = jnp.dot(t_ladder, vvvv_blk, preferred_element_type=jnp.float32)
        t_cols = lax.all_gather(t_half, "row", axis=0, tiled=True)
        x_part = lax.dot_general(oovv_blk, t_cols, (((1,), (1,)), ((), ())), preferred_element_type=jnp.float32)
        x_rows = lax.psum(x_part, "col")
        row_idx = lax.axis_index("row")
        oooo_rows = lax.dynamic_slice_in_dim(oooo_full, row_idx * rows_dev, rows_dev, axis=0)
        hole_mat = (oooo_rows.astype(jnp.float32) + 0.5 * x_rows).astype(jnp.bfloat16)
        hole_part = lax.dot_general(hole_mat, t_half, (((0,), (0,)), ((), ())), preferred_element_type=jnp.float32)
        ladder_sum = lax.psum_scatter(ladder_part + hole_part, "row", scatter_dimension=0, tiled=True)
        t_four = t_rows.reshape(occ_row, n_occ, n_virt, n_virt)
        direct_term = jnp.einsum("ikac,kcjb->ijab", t_four, wd_blk.reshape(n_occ, n_virt, occ_col, n_virt), preferred_element_type=jnp.float32)
        exch_term = jnp.einsum("ikcb,kcja->ijab", t_four, wx_blk.reshape(n_occ, n_virt, occ_col, n_virt), preferred_element_type=jnp.float32)
        ph_back = lax.all_to_all(direct_term - exch_term, "col", 2, 1, tiled=True)
        swap_row = lax.all_to_all(ph_back, "row", 1, 0, tiled=True)
        swap_both = lax.all_to_all(swap_row, "col", 3, 2, tiled=True)
        ph_sym = (ph_back + swap_both.transpose(1, 0, 3, 2)).reshape(rows_dev, cols_dev)
        residual = oovv_blk.astype(jnp.float32) + ladder_sum + ph_sym
        return residual / d_blk

    return jax.shard_map(local_sweep, mesh=mesh, in_specs=(amp_spec, amp_spec, amp_spec, amp_spec, P(), wide_spec, wide_spec), out_specs=amp_spec, check_vma=False)
```

profile of v0, /device:TPU:0, one launch (start us, length us, event | category | flops | bytes accessed | tf_op | source)
XLA Modules:
  0.0 230.4 jit_solution(4782694283009717438)
XLA Ops:
  6.5 0.0 all-gather.5.cloned.1.call-start
  6.5 2.4 %copy.27 = bf16[128,2304]{0,1:T(8,128)(2,1)} copy(f32[128,2304]{1,0:T(8,128)} %param.7) | data formatting | bytes 1769472 | tf_op args[0]
  8.9 0.0 all-gather.5.cloned.1.call-update
  9.0 0.0 all-reduce.2.cloned.1.call-start
  9.0 8.9 %all-gather.5.cloned.1.call-done = bf16[256,2304]{0,1:T(8,128)(2,1)} async-done(((bf16[128,2304]{0,1:T(8,128)(2,1)}), bf16[256,2304]{0,1:T(8,128)(2,1)}) %all-gather.5.cloned.1.call-update) | async-done | bytes 1179664 | tf_op jit(solution)/shard_map/all_gather | solution.py:24
  17.9 0.0 copy-done.2
  17.9 2.3 fusion.11
  20.2 0.0 all-reduce.2.cloned.1.call-update
  20.2 0.0 all-gather.3.cloned.1.call-start
  20.3 0.7 all-gather.3.cloned.1.call-update
  20.9 0.0 reduce-scatter.2.cloned.1.call-start
  21.0 31.8 %all-reduce.2.cloned.1.call-done = f32[128,256]{1,0:T(8,128)} async-done(((f32[128,256]{1,0:T(8,128)}), f32[128,256]{1,0:T(8,128)}) %all-reduce.2.cloned.1.call-update) | async-done | bytes 131088 | tf_op jit(solution)/shard_map/psum | solution.py:26
  52.8 0.0 copy-done.1
  52.8 0.0 copy-done.6
  52.9 2.8 %fusion.6 = f32[256,2304]{1,0:T(8,128)} fusion(bf16[128,2304]{0,1:T(8,128)(2,1)S(1)} %copy-done.1, f32[128,256]{1,0:T(8,128)} %all-reduce.2.cloned.1.call-done, bf16[256,256]{1,0:T(8,128)(2,1)S(1)} %copy-done.6, s32[]{:T(128)S(6)} %select_n.3), kind=kOutput, calls=%fused_computation.10 | convolution fusion | flops 151126016 | bytes 3145732 | tf_op jit(solution)/shard_map/dot_general | solution.py:30
  55.7 30.5 %all-gather.3.cloned.1.call-done = bf16[128,9216]{0,1:T(8,128)(2,1)} async-done(((bf16[128,2304]{0,1:T(8,128)(2,1)}), bf16[128,9216]{0,1:T(8,128)(2,1)}) %all-gather.3.cloned.1.call-update) | async-done | bytes 2359312 | tf_op jit(solution)/shard_map/all_gather | solution.py:21
  86.2 6.7 %all_to_all.73 = bf16[128,2,4608]{0,2,1:T(8,128)(2,1)S(1)} all-to-all(bf16[128,2,4608]{0,2,1:T(8,128)(2,1)} %bitcast.47), channel_id=1, replica_groups=mesh['col'=4,'row'=2] {'row'}, dimensions={1} | all-to-all | bytes 4718592 | tf_op jit(solution)/shard_map/all_to_all | solution.py:22
  92.8 2.6 %copy.28 = bf16[2,128,4608]{2,1,0:T(8,128)(2,1)} copy(bf16[2,128,4608]{1,2,0:T(8,128)(2,1)S(1)} %bitcast.48) | data formatting | bytes 4718592 | tf_op jit(solution)/shard_map/all_to_all | solution.py:22
  95.4 14.6 %convolution_add_fusion = f32[256,2304]{1,0:T(8,128)} fusion(f32[256,2304]{1,0:T(8,128)} %fusion.6, bf16[256,4608]{1,0:T(8,128)(2,1)} %bitcast.52, bf16[4608,2304]{1,0:T(8,128)(2,1)} %param.10), kind=kOutput, calls=%fused_computation.1 | convolution fusion | flops 5436407808 | bytes 28311552 | tf_op jit(solution)/shard_map/dot_general | solution.py:23
  110.0 0.0 reduce-scatter.2.cloned.1.call-update
  110.1 1.2 copy-done.4
  111.3 2.1 reshape.15
  113.4 0.0 copy-done.5
  113.4 2.1 reshape.17
  115.5 0.0 copy-done
  115.5 2.5 %copy.29 = bf16[128,9216]{1,0:T(8,128)(2,1)} copy(bf16[128,9216]{0,1:T(8,128)(2,1)S(1)} %copy-done) | data formatting | bytes 4718592 | tf_op jit(solution)/shard_map/all_gather | solution.py:21
  118.0 4.5 %reshape.20 = bf16[8,16,96,96,1]{3,2,1,0,4:T(8,128)(2,1)S(1)} reshape(bf16[128,9216]{1,0:T(8,128)(2,1)} %copy.29) | data formatting | bytes 4718592 | tf_op jit(solution)/shard_map/reshape | solution.py:32
  122.4 0.0 copy-start.3
  122.4 3.0 %fusion = f32[4,96,8,96,1]{1,3,4,2,0:T(8,128)S(1)} fusion(bf16[8,16,96,96,1]{3,2,1,0,4:T(8,128)(2,1)S(1)} %reshape.20, bf16[16,96,4,96,1]{3,2,1,0,4:T(4,128)(2,1)} %bitcast.54), kind=kOutput, calls=%fused_computation.4 | convolution fusion | flops 905969664 | bytes 4718592 | tf_op jit(solution)/shard_map/ikcb,kcja->ijab/dot_general | solution.py:34
  125.5 3.0 %bitcast_subtract_fusion = f32[8,4,96,96]{2,3,0,1:T(8,128)} fusion(f32[4,96,8,96,1]{1,3,4,2,0:T(8,128)S(1)} %fusion, bf16[8,16,96,96,1]{3,2,1,0,4:T(8,128)(2,1)S(1)} %reshape.20, bf16[16,96,4,96,1]{3,2,1,0,4:T(4,128)(2,1)S(1)} %bitcast.53), kind=kOutput, calls=%fused_computation.2 | convolution fusion | flops 906264576 | bytes 5898240 | tf_op jit(solution)/shard_map/ikac,kcjb->ijab/dot_general | solution.py:33
  128.5 2.8 %copy.33 = f32[8,4,96,96]{3,0,1,2:T(8,128)S(1)} copy(f32[8,4,96,96]{2,3,0,1:T(8,128)} %bitcast_subtract_fusion) | data formatting | bytes 2359296 | tf_op jit(solution)/shard_map/sub | solution.py:35
  131.3 22.8 %all_to_all.74 = f32[8,4,96,96]{3,0,1,2:T(8,128)S(1)} all-to-all(f32[8,4,96,96]{3,0,1,2:T(8,128)S(1)} %copy.33), channel_id=1, replica_groups=mesh['col'=4,'row'=2] {'col'}, dimensions={2} | all-to-all | bytes 2359296 | tf_op jit(solution)/shard_map/all_to_all | solution.py:35
  154.1 0.9 copy.35
  155.0 0.2 copy.36
  155.1 5.0 %all_to_all.75 = f32[8,16,24,96]{3,2,0,1:T(8,128)S(1)} all-to-all(f32[8,16,24,96]{3,2,0,1:T(8,128)S(1)} %copy.36), channel_id=1, replica_groups=mesh['col'=4,'row'=2] {'row'}, dimensions={1} | all-to-all | bytes 2359296 | tf_op jit(solution)/shard_map/all_to_all | solution.py:36
  160.2 0.2 copy.38
  160.3 4.6 %copy.39 = f32[16,8,24,96]{2,1,0,3:T(8,128)} copy(f32[16,8,24,96]{3,2,1,0:T(8,128)S(1)} %bitcast.51) | data formatting | bytes 2359296 | tf_op jit(solution)/shard_map/all_to_all | solution.py:36
  164.9 6.5 %reshape.25 = f32[4,1,73728]{2,1,0:T(1,128)S(1)} reshape(f32[96,16,8,24]{3,2,1,0:T(8,128)} %bitcast.43) | data formatting | bytes 2359296
  171.4 19.2 %all_to_all.76 = f32[4,1,73728]{2,1,0:T(1,128)} all-to-all(f32[4,1,73728]{2,1,0:T(1,128)S(1)} %reshape.25), channel_id=1, replica_groups=mesh['col'=4,'row'=2] {'col'}, dimensions={0} | all-to-all | bytes 2359296 | tf_op jit(solution)/shard_map/all_to_all | solution.py:37
  190.6 0.5 broadcast
  191.1 5.0 %reduce = f32[4,73728]{1,0:T(4,128)S(1)} reduce(f32[4,1,73728]{2,1,0:T(1,128)} %all_to_all.76, f32[]{:T(128)} %broadcast), dimensions={1}, to_apply=%all_to_all.65.reduce_sub_computation | reduce | bytes 2359300 | tf_op jit(solution)/shard_map/all_to_all | solution.py:37
  196.1 7.4 %reshape.26 = f32[96,16,8,24]{3,2,1,0:T(8,128)} reshape(f32[4,73728]{1,0:T(4,128)S(1)} %reduce) | data formatting | bytes 2359296
  203.5 9.5 %copy.64 = f32[16,8,24,4,24]{2,3,4,1,0:T(4,128)} copy(f32[16,8,24,4,24]{2,1,0,4,3:T(8,128)} %bitcast.42) | data formatting | bytes 2359296 | tf_op jit(solution)/shard_map/all_to_all | solution.py:37
  213.0 5.8 %all_to_all.68 = f32[16,8,96,24]{2,3,1,0:T(8,128)} reshape(f32[16,8,4,24,24]{3,2,4,1,0:T(4,128)} %bitcast.44) | data formatting | bytes 2359296 | tf_op jit(solution)/shard_map/all_to_all | solution.py:37
  218.8 1.6 bitcast_add_fusion
  220.3 0.5 reshape.18
  220.8 0.0 reduce-scatter.2.cloned.1.call-done
  220.9 3.0 %add_divide_fusion = f32[128,2304]{1,0:T(8,128)} fusion(f32[128,2304]{1,0:T(8,128)} %param.8, f32[128,2304]{1,0:T(8,128)S(1)} %reshape.18, f32[128,2304]{1,0:T(8,128)} %reduce-scatter.2.cloned.1.call-done, bf16[128,2304]{1,0:T(8,128)(2,1)} %param.9), kind=kLoop, calls=%fused_computation.8 | loop fusion | flops 1179648 | bytes 5308416 | tf_op jit(solution)/shard_map/div | solution.py:40
  (7 shorter events, 0.0 us)
Async XLA Ops:
  6.5 11.4 %copy-start.2 = (bf16[128,2304]{1,0:T(8,128)(2,1)S(1)}, bf16[128,2304]{1,0:T(8,128)(2,1)}, u32[]{:S(2)}) copy-start(bf16[128,2304]{1,0:T(8,128)(2,1)} %param.9) | copy-start | bytes 1769476
  6.5 11.4 %all-gather.5.cloned.1.call-start = ((), (), s32[]{:S(2)}) async-start(), calls=%async_computation.6 | async-start | bytes 1769472 | tf_op jit(solution)/shard_map/all_gather | solution.py:24
  8.9 43.9 %copy-start.1 = (bf16[128,2304]{0,1:T(8,128)(2,1)S(1)}, bf16[128,2304]{0,1:T(8,128)(2,1)}, u32[]{:S(2)}) copy-start(bf16[128,2304]{0,1:T(8,128)(2,1)} %copy.27) | copy-start | bytes 1769476
  8.9 43.9 %copy-start.6 = (bf16[256,256]{1,0:T(8,128)(2,1)S(1)}, bf16[256,256]{1,0:T(8,128)(2,1)}, u32[]{:S(2)}) copy-start(bf16[256,256]{1,0:T(8,128)(2,1)} %param.11) | copy-start | bytes 393220
  9.0 43.9 %all-reduce.2.cloned.1.call-start = ((), (), s32[]{:S(2)}) async-start(), calls=%async_computation.7 | async-start | bytes 262144 | tf_op jit(solution)/shard_map/psum | solution.py:26
  20.2 65.9 %all-gather.3.cloned.1.call-start = ((), (), s32[]{:S(2)}) async-start(), calls=%async_computation.5 | async-start | bytes 2949120 | tf_op jit(solution)/shard_map/all_gather | solution.py:21
  20.9 199.9 %reduce-scatter.2.cloned.1.call-start = ((), (), s32[]{:S(2)}) async-start(), calls=%async_computation.8 | async-start | bytes 3538944 | tf_op jit(solution)/shard_map/reduce_scatter | solution.py:31
  110.0 1.3 copy-start.4
  111.3 2.1 copy-start.5
  113.4 2.1 copy-start
  122.4 3.0 %copy-start.3 = (bf16[16,96,4,96]{3,2,1,0:T(4,128)(2,1)S(1)}, bf16[16,96,4,96]{3,2,1,0:T(4,128)(2,1)}, u32[]{:S(2)}) copy-start(bf16[16,96,4,96]{3,2,1,0:T(4,128)(2,1)} %reshape.15) | copy-start | bytes 3538948
Sparse Core Ops, SparseCore 0:
  9.1 8.8 all-gather.4
  20.8 32.0 all-reduce.1
  54.6 31.4 all-gather.2
  110.2 6.7 reduce-scatter.1
where the time goes:
time: 231 us; the launch traced here: 230 us
  waiting for transfers between devices  72 us (31%)
  local copies, waits for them, and re-layouts  56.1 us (24%)
  blocking collectives  53.6 us (23%)
  matrix products  25.7 us (11%)
  between operations  13.2 us (6%)
  other arithmetic  9.56 us (4%)
    psum x1, waiting for transfers between devices, local_sweep(): x_rows = lax.psum(x_part, 'col')  31.8 us
    all_gather x1, waiting for transfers between devices, local_sweep(): t_rows = lax.all_gather(t_half, 'col', axis=1, tiled=True)  30.5 us
    all_to_all x1, blocking collectives, local_sweep(): ph_back = lax.all_to_all(direct_term - exch_term, 'col', 2, 1, tiled=True)  22.8 us
    all_to_all x1, blocking collectives, local_sweep(): swap_both = lax.all_to_all(swap_row, 'col', 3, 2, tiled=True)  19.2 us
    unnamed x17, local copies, waits for them, and re-layouts  17.5 us
    all_to_all x3, local copies, waits for them, and re-layouts, local_sweep(): swap_both = lax.all_to_all(swap_row, 'col', 3, 2, tiled=True)  15.8 us
    dot_general x1, matrix products, local_sweep(): jnp.dot(t_ladder, vvvv_blk, preferred_element_type=jnp.float32)  14.6 us
    all_gather x1, waiting for transfers between devices, local_sweep(): t_cols = lax.all_gather(t_half, 'row', axis=0, tiled=True)  8.92 us
  transfers between devices with their start and end apart: 4, of which 3 were waited for; matrix products, arithmetic and copies ran while one was open for 26% of the time, Pallas kernels for 0%

commit v1 on v0

v1 whole, which is shorter than its diff:
```python
import functools

import jax
import jax.numpy as jnp
from jax import lax
from jax.experimental import pallas as pl
from jax.experimental.pallas import tpu as pltpu
from jax.sharding import PartitionSpec as P

MESH = pl.DeviceIdType.MESH
F32 = jnp.float32
BF16 = jnp.bfloat16
NT = (((1,), (1,)), ((), ()))
TN = (((0,), (0,)), ((), ()))


def _place():
    r, c = lax.axis_index("row"), lax.axis_index("col")
    x, y = c % 2, c // 2
    return r, c, y * 2 + (1 - x), (1 - y) * 2 + x, (1 - y) * 2 + (1 - x)


def _dev(c, r):
    return {"col": c, "row": r}


def _barrier(r, c, nx, ny, dg):
    sem = pltpu.get_barrier_semaphore()
    o = 1 - r
    for cc, rr in ((nx, r), (ny, r), (dg, r), (c, o), (nx, o), (ny, o), (dg, o)):
        pl.semaphore_signal(sem, inc=1, device_id=_dev(cc, rr), device_id_type=MESH)
    pl.semaphore_wait(sem, 7)


def _rcopy(src, dst, ssem, rsem, dev):
    return pltpu.make_async_remote_copy(src, dst, ssem, rsem, device_id=dev, device_id_type=MESH)


def gather_kernel(t_ref, oovv_ref, oooo_ref, rows_out, lad_out, hole_out,
                  tg, xp, xr, mfull, hole, ssem, rsem, xs, xrs, ms, mrs, osem):
    r, c, nx, ny, dg = _place()
    o = 1 - r
    n = t_ref.shape[0]
    w = t_ref.shape[1]
    h = w // 2
    rows = pl.ds(pl.multiple_of(r * n, n), n)
    orows = pl.ds(pl.multiple_of(o * n, n), n)
    h0, h1 = pl.ds(0, h), pl.ds(h, h)
    _barrier(r, c, nx, ny, dg)

    d_own = _rcopy(t_ref, tg.at[c, rows], ssem.at[0], rsem.at[0], _dev(c, o))
    x0 = _rcopy(t_ref.at[:, h0], tg.at[c, rows, h0], ssem.at[1], rsem.at[1], _dev(nx, r))
    y1 = _rcopy(t_ref.at[:, h1], tg.at[c, rows, h1], ssem.at[2], rsem.at[2], _dev(ny, r))
    x1 = _rcopy(t_ref.at[:, h1], tg.at[c, rows, h1], ssem.at[3], rsem.at[3], _dev(nx, r))
    y0 = _rcopy(t_ref.at[:, h0], tg.at[c, rows, h0], ssem.at[4], rsem.at[4], _dev(ny, r))
    d_own.start()
    x0.start()
    y1.start()
    tg[c, rows, :] = t_ref[...]

    d_own.wait_recv()
    xp[...] = lax.dot_general(oovv_ref[...], tg[c], NT, preferred_element_type=F32)
    q = n // 4
    xcopies = []
    for s, cc in enumerate((nx, ny, dg)):
        cp = _rcopy(xp.at[pl.ds(pl.multiple_of(cc * q, q), q)], xr.at[c], xs.at[s], xrs.at[s], _dev(cc, r))
        cp.start()
        xcopies.append(cp)
    x1.start()
    y0.start()
    piece = pl.ds(pl.multiple_of(c * q, q), q)
    xr[c, :, :] = xp[piece, :]
    for cp in xcopies:
        cp.wait_recv()
    xsum = (xr[0] + xr[1]) + (xr[2] + xr[3])
    krows = pl.ds(pl.multiple_of(r * n + c * q, q), q)
    mfull[krows, :] = (oooo_ref[krows, :].astype(F32) + 0.5 * xsum).astype(BF16)
    mcopies = []
    for s, (cc, rr) in enumerate(((nx, r), (ny, r), (dg, r), (c, o), (nx, o), (ny, o), (dg, o))):
        cp = _rcopy(mfull.at[krows], mfull.at[krows], ms.at[s], mrs.at[s], _dev(cc, rr))
        cp.start()
        mcopies.append(cp)

    x0.wait_recv()
    f0 = _rcopy(tg.at[nx, rows, h0], tg.at[nx, rows, h0], ssem.at[5], rsem.at[5], _dev(ny, r))
    f0.start()
    y1.wait_recv()
    f1 = _rcopy(tg.at[ny, rows, h1], tg.at[ny, rows, h1], ssem.at[6], rsem.at[6], _dev(nx, r))
    f1.start()
    x1.wait_recv()
    d_x = _rcopy(tg.at[nx, rows], tg.at[nx, rows], ssem.at[7], rsem.at[7], _dev(c, o))
    d_x.start()
    y0.wait_recv()
    d_y = _rcopy(tg.at[ny, rows], tg.at[ny, rows], ssem.at[8], rsem.at[8], _dev(c, o))
    d_y.start()

    for cp in mcopies:
        cp.wait_recv()
    m_mine = mfull[:, rows]
    step = 256

    @pl.loop(0, w // step)
    def _(s):
        lanes = pl.ds(pl.multiple_of(s * step, step), step)
        hole[:, lanes] = lax.dot_general(m_mine, tg[c, :, lanes], TN, preferred_element_type=F32)

    f0.wait_recv()
    f1.wait_recv()
    d_d = _rcopy(tg.at[dg, rows], tg.at[dg, rows], ssem.at[9], rsem.at[9], _dev(c, o))
    d_d.start()
    outs = [pltpu.make_async_copy(hole, hole_out, osem.at[0])]
    for cc in range(4):
        outs.append(pltpu.make_async_copy(tg.at[cc, rows], rows_out.at[:, pl.ds(cc * w, w)], osem.at[1 + cc]))
    for cp in outs:
        cp.start()
    d_x.wait_recv()
    d_y.wait_recv()
    d_d.wait_recv()
    for p in range(2):
        cp = pltpu.make_async_copy(tg.at[2 * r + p], lad_out.at[:, pl.ds(p * w, w)], osem.at[5 + p])
        cp.start()
        outs.append(cp)
    for cp in (d_own, x0, y1, x1, y0, f0, f1, d_x, d_y, d_d, *xcopies, *mcopies):
        cp.wait_send()
    for cp in outs:
        cp.wait()


def exchange_kernel(s_ref, p_ref, t_ref, v_ref, hole_ref, oovv_ref, den_ref, out_ref,
                    srecv, precv, vbuf, tl, mine, theirs, sbuf, ss, srs, ps, prs, vsem, tsem, rs, rrs, lsem):
    r, c, nx, ny, dg = _place()
    o = 1 - r
    w = out_ref.shape[1]
    n = out_ref.shape[0]
    step = vbuf.shape[2]
    steps = w // step
    tload = pltpu.make_async_copy(t_ref, tl, tsem)
    tload.start()

    def vcopy(s, slot):
        lanes = pl.ds(pl.multiple_of(s * step, step), step)
        return pltpu.make_async_copy(v_ref.at[:, lanes], vbuf.at[slot], vsem.at[slot])

    vcopy(0, 0).start()
    vcopy(1, 1).start()
    _barrier(r, c, nx, ny, dg)

    def cols(cc):
        return pl.ds(pl.multiple_of(cc * w, w), w)

    own = c // 2
    half = c % 2
    copies = []
    for s, cc in enumerate((dg, nx, ny)):
        copies.append(_rcopy(s_ref.at[:, :, cols(cc)], srecv.at[c], ss.at[s], srs.at[c], _dev(cc, r)))
        copies.append(_rcopy(p_ref.at[:, :, cols(cc)], precv.at[half, r], ps.at[s], prs.at[half, r], _dev(cc, own)))
    for cp in copies:
        cp.start()
    local = pltpu.make_async_copy(s_ref.at[:, :, cols(c)], srecv.at[c], srs.at[c])
    local.start()
    p_near = pltpu.make_async_copy(p_ref.at[:, :, cols(c)], precv.at[half, r], prs.at[half, r])
    p_far = _rcopy(p_ref.at[:, :, cols(c)], precv.at[half, r], ps.at[3], prs.at[half, r], _dev(c, own))

    @pl.when(own == r)
    def _():
        p_near.start()

    @pl.when(own != r)
    def _():
        p_far.start()

    tload.wait()

    def half_rows(k):
        return pl.ds(pl.multiple_of(k * n, n), n)

    def ladder_copy(s):
        lanes = pl.ds(pl.multiple_of(s * step, step), step)
        return _rcopy(sbuf.at[s], theirs.at[:, lanes], rs.at[s], rrs.at[s], _dev(c, o))

    @pl.loop(0, steps)
    def _(s):
        slot = s % 3

        @pl.when(s + 2 < steps)
        def _():
            vcopy(s + 2, (s + 2) % 3).start()

        vcopy(s, slot).wait()
        lanes = pl.ds(pl.multiple_of(s * step, step), step)
        vb = vbuf.at[slot]
        sbuf[s, :, :] = jnp.dot(tl[half_rows(o), :], vb[...], preferred_element_type=F32)
        ladder_copy(s).start()
        mine[:, lanes] = jnp.dot(tl[half_rows(r), :], vb[...], preferred_element_type=F32)

    @pl.loop(0, steps)
    def _(s):
        ladder_copy(s).wait()

    for cc in range(4):
        pltpu.make_async_copy(s_ref.at[:, :, cols(c)], srecv.at[cc], srs.at[cc]).wait()
    for a in range(2):
        for b in range(2):
            pltpu.make_async_copy(p_ref.at[:, :, cols(c)], precv.at[a, b], prs.at[a, b]).wait()
    for cp in copies:
        cp.wait_send()

    @pl.when(own != r)
    def _():
        p_far.wait_send()

    nb = precv.shape[2]
    for i in range(srecv.shape[1]):
        line = pl.ds(i * 16, 16)
        sv = jnp.concatenate([srecv[cc, i] for cc in range(4)], axis=0)
        pv = jnp.concatenate([precv[i // nb, b, i % nb] for b in range(2)], axis=0)
        total = oovv_ref[line, :].astype(F32) + (mine[line, :] + theirs[line, :] + hole_ref[line, :]) + (sv + pv)
        out_ref[line, :] = total / den_ref[line, :]


VM = pl.BlockSpec(memory_space=pltpu.VMEM)
ANY = pl.BlockSpec(memory_space=pl.ANY)
DMA = pltpu.SemaphoreType.DMA


def gather(t_half, oovv, oooo):
    n, w = t_half.shape
    return pl.pallas_call(
        gather_kernel,
        out_shape=(
            jax.ShapeDtypeStruct((n, 4 * w), BF16),
            jax.ShapeDtypeStruct((2 * n, 2 * w), BF16),
            jax.ShapeDtypeStruct((n, w), F32),
        ),
        in_specs=[VM, VM, VM],
        out_specs=(ANY, ANY, ANY),
        scratch_shapes=[
            pltpu.VMEM((4, 2 * n, w), BF16),
            pltpu.VMEM((n, 2 * n), F32),
            pltpu.VMEM((4, n // 4, 2 * n), F32),
            pltpu.VMEM((2 * n, 2 * n), BF16),
            pltpu.VMEM((n, w), F32),
            DMA((10,)), DMA((10,)), DMA((3,)), DMA((3,)), DMA((7,)), DMA((7,)), DMA((7,)),
        ],
        compiler_params=pltpu.CompilerParams(collective_id=0, has_side_effects=True, vmem_limit_bytes=40 << 20),
        name="gather",
    )(t_half, oovv, oooo)


def exchange(s_parts, p_parts, t_lad, vvvv, hole, oovv, den):
    n, w = den.shape
    step = 256
    steps = w // step
    depth = vvvv.shape[0]
    return pl.pallas_call(
        exchange_kernel,
        out_shape=jax.ShapeDtypeStruct((n, w), F32),
        in_specs=[ANY, ANY, ANY, ANY, VM, VM, VM],
        out_specs=VM,
        scratch_shapes=[
            pltpu.VMEM((4, 8, 4, w), F32),
            pltpu.VMEM((2, 2, 4, 8, w), F32),
            pltpu.VMEM((3, depth, step), BF16),
            pltpu.VMEM((2 * n, depth), BF16),
            pltpu.VMEM((n, w), F32),
            pltpu.VMEM((n, w), F32),
            pltpu.VMEM((steps, n, step), F32),
            DMA((3,)), DMA((4,)), DMA((4,)), DMA((2, 2)), DMA((3,)), DMA, DMA((steps,)), DMA((steps,)), DMA,
        ],
        compiler_params=pltpu.CompilerParams(collective_id=1, has_side_effects=True, vmem_limit_bytes=60 << 20),
        name="exchange",
    )(s_parts, p_parts, t_lad, vvvv, hole, oovv, den)


def solution(mesh):
    def local_sweep(t_blk, d_blk, oovv_blk, vvvv_blk, oooo_full, wd_blk, wx_blk):
        t_half = t_blk.astype(BF16)
        t_rows, t_lad, hole = gather(t_half, oovv_blk, oooo_full)
        t_four = t_rows.reshape(8, 16, 96, 96)
        direct = jnp.einsum("ikac,kcjb->ijab", t_four, wd_blk.reshape(16, 96, 4, 96), preferred_element_type=F32)
        exch = jnp.einsum("ikcb,kcja->ijab", t_four, wx_blk.reshape(16, 96, 4, 96), preferred_element_type=F32)
        s = direct - exch
        s_parts = s.reshape(8, 4, 9216)
        p_parts = s.transpose(1, 0, 3, 2).reshape(4, 8, 9216)
        return exchange(s_parts, p_parts, t_lad, vvvv_blk, hole, oovv_blk, d_blk)

    amp = P("row", "col")
    wide = P(None, "col")
    return jax.shard_map(local_sweep, mesh=mesh, in_specs=(amp, amp, amp, amp, P(), wide, wide), out_specs=amp, check_vma=False)
```

time: 231 us -> 100 us (0.43)
  waiting for transfers between devices: 72 us -> 0 us
  Pallas kernels: 0 us -> 62.6 us
  blocking collectives: 53.6 us -> 0 us
  local copies, waits for them, and re-layouts: 56.1 us -> 25.7 us
  matrix products: 25.7 us -> 8.73 us
  between operations: 13.2 us -> 0.06 us
  other arithmetic: 9.56 us -> 2.8 us
    pallas_call x0 -> x2, Pallas kernels: none -> 62.6 us  [the longest x1 32.9 us: exchange(): pl.pallas_call(exchange_kernel, out_shape=jax.ShapeDtypeStruct((n, w), F3...]
    all_to_all x4 -> x0, blocking collectives: 53.6 us -> none  [the longest x1 22.8 us: local_sweep(): ph_back = lax.all_to_all(direct_term - exch_term, 'col', 2, 1, tiled=True)]
    all_gather x2 -> x0, waiting for transfers between devices: 39.4 us -> none  [the longest x1 30.5 us: local_sweep(): t_rows = lax.all_gather(t_half, 'col', axis=1, tiled=True)]
    psum x1 -> x0, waiting for transfers between devices: 31.8 us -> none  [local_sweep(): x_rows = lax.psum(x_part, 'col')]
    all_to_all x8 -> x0, local copies, waits for them, and re-layouts: 24.2 us -> none  [the longest x3 15.8 us: local_sweep(): swap_both = lax.all_to_all(swap_row, 'col', 3, 2, tiled=True)]
    dot_general x5 -> x2, matrix products: 25.7 us -> 8.73 us  [the longest x1 4.95 us: local_sweep(): jnp.einsum('ikac,kcjb->ijab', t_four, wd_blk.reshape(16, 96, 4, 96), pref...]
    unnamed x17 -> x13, local copies, waits for them, and re-layouts: 17.5 us -> 4.99 us
    reshape x4 -> x6, local copies, waits for them, and re-layouts: 9.12 us -> 18.8 us  [the longest x2 8.23 us: local_sweep(): t_four = t_rows.reshape(8, 16, 96, 96)]
  transfers between devices with their start and end apart: 4 -> 0, of which waited for: 3 -> 0; matrix products, arithmetic and copies ran while one was open for 26% -> 0% of each run, Pallas kernels for 0% -> 0%
where the time goes in v1:
time: 100 us; the launch traced here: 99.9 us
  Pallas kernels  62.6 us (63%)
  local copies, waits for them, and re-layouts  25.7 us (26%)
  matrix products  8.73 us (9%)
  other arithmetic  2.8 us (3%)
    pallas_call x1, Pallas kernels, exchange(): pl.pallas_call(exchange_kernel, out_shape=jax.ShapeDtypeStruct((n, w), F3...  32.9 us
    pallas_call x1, Pallas kernels, gather(): pl.pallas_call(gather_kernel, out_shape=(jax.ShapeDtypeStruct((n, 4 * w),...  29.7 us
    reshape x2, local copies, waits for them, and re-layouts, local_sweep(): t_four = t_rows.reshape(8, 16, 96, 96)  8.23 us
    unnamed x13, local copies, waits for them, and re-layouts  4.99 us
    dot_general x1, matrix products, local_sweep(): jnp.einsum('ikac,kcjb->ijab', t_four, wd_blk.reshape(16, 96, 4, 96), pref...  4.95 us
    reshape x1, local copies, waits for them, and re-layouts, local_sweep(): wx_blk.reshape(16, 96, 4, 96)  4.38 us
    dot_general x1, matrix products, local_sweep(): jnp.einsum('ikcb,kcja->ijab', t_four, wx_blk.reshape(16, 96, 4, 96), pref...  3.78 us
    reshape x1, local copies, waits for them, and re-layouts, local_sweep(): wd_blk.reshape(16, 96, 4, 96)  2.15 us

profile of v1, /device:TPU:0, one launch (start us, length us, event | category | flops | bytes accessed | tf_op | source)
XLA Modules:
  0.0 99.9 jit_solution(12760781574021461139)
XLA Ops:
  0.0 0.0 copy-start.3
  0.0 0.0 copy-start.1
  0.0 1.4 %convert_element_type.3.t_ref = bf16[128,2304]{1,0:T(8,128)(2,1)S(1)} convert(f32[128,2304]{1,0:T(8,128)} %param.7) | non-fusion elementwise | flops 294912 | bytes 1769472 | tf_op jit(solution)/shard_map/convert_element_type | solution.py:277
  1.4 0.0 copy-done.3
  1.4 0.1 copy-done.1
  1.5 29.7 %gather.1 = (bf16[128,9216]{1,0:T(8,128)(2,1)S(1)}, bf16[256,4608]{1,0:T(8,128)(2,1)S(1)}, f32[128,2304]{1,0:T(8,128)S(1)}) custom-call(bf16[128,2304]{1,0:T(8,128)(2,1)S(1)} %convert_element_type.3.t_ref, bf16[128,2304]{1,0:T(8,128)(2,1)S(1)} %copy-done.1, bf16[256,256]{1,0:T(8,128)(2,1)S(1)} %copy-done.3), custom_call_target="tpu_custom_call" | custom-call | tf_op jit(solution)/shard_map/gather/pallas_call | solution.py:228
  31.2 0.0 copy-start
  31.2 1.4 %copy-done = bf16[256,4608]{1,0:T(8,128)(2,1)} copy-done((bf16[256,4608]{1,0:T(8,128)(2,1)}, bf16[256,4608]{1,0:T(8,128)(2,1)S(1)}, u32[]{:S(2)}) %copy-start) | copy-done | bytes 2359320
  32.6 0.0 copy-start.2
  32.6 1.1 %copy-done.2 = f32[128,2304]{1,0:T(8,128)} copy-done((f32[128,2304]{1,0:T(8,128)}, f32[128,2304]{1,0:T(8,128)S(1)}, u32[]{:S(2)}) %copy-start.2) | copy-done | bytes 1179672
  33.7 0.0 copy-start.5
  33.7 4.1 %reshape.20 = bf16[8,16,96,96,1]{3,2,1,0,4:T(8,128)(2,1)} reshape(bf16[128,9216]{1,0:T(8,128)(2,1)S(1)} %get-tuple-element.8) | data formatting | bytes 4718592 | tf_op jit(solution)/shard_map/reshape | solution.py:279
  37.8 0.0 copy-done.5
  37.8 2.1 %reshape.16 = bf16[16,96,4,96]{3,2,1,0:T(4,128)(2,1)} reshape(bf16[1536,384]{1,0:T(8,128)(2,1)S(1)} %copy-done.5) | data formatting | bytes 2359296 | tf_op jit(solution)/shard_map/reshape | solution.py:280
  40.0 5.0 %fusion.2 = f32[8,96,4,96,1]{3,1,4,2,0:T(8,128)} fusion(bf16[8,16,96,96,1]{3,2,1,0,4:T(8,128)(2,1)} %reshape.20, bf16[16,96,4,96]{3,2,1,0:T(4,128)(2,1)} %reshape.16), kind=kOutput, calls=%fused_computation.2 | convolution fusion | flops 905969664 | bytes 4718592 | tf_op jit(solution)/shard_map/ikac,kcjb->ijab/dot_general | solution.py:280
  44.9 4.1 %reshape.15 = bf16[8,16,96,96]{3,2,1,0:T(8,128)(2,1)} reshape(bf16[128,9216]{1,0:T(8,128)(2,1)S(1)} %get-tuple-element.8) | data formatting | bytes 4718592 | tf_op jit(solution)/shard_map/reshape | solution.py:279
  49.1 0.0 copy-start.4
  49.1 4.4 %reshape.17 = bf16[16,96,4,96]{3,2,1,0:T(4,128)(2,1)} reshape(bf16[1536,384]{1,0:T(8,128)(2,1)} %param.13) | data formatting | bytes 2359296 | tf_op jit(solution)/shard_map/reshape | solution.py:281
  53.4 0.0 copy-done.4
  53.5 3.8 %bitcast_subtract_fusion.1 = (f32[8,4,96,96]{3,2,1,0:T(8,128)S(1)}, f32[8,96,4,96,1]{1,3,4,2,0:T(8,128)S(1)}) fusion(f32[8,96,4,96,1]{3,1,4,2,0:T(8,128)S(1)} %copy-done.4, bf16[16,96,4,96]{3,2,1,0:T(4,128)(2,1)} %reshape.17, bf16[8,16,96,96]{3,2,1,0:T(8,128)(2,1)} %reshape.15), kind=kOutput, calls=%fused_computation.5 | convolution fusion | flops 906264576 | bytes 7077888 | tf_op jit(solution)/shard_map/ikcb,kcja->ijab/dot_general | solution.py:281
  57.2 1.4 %bitcast_subtract_fusion = f32[4,8,96,96]{2,3,0,1:T(8,128)} fusion(f32[8,96,4,96,1]{1,3,4,2,0:T(8,128)S(1)} %get-tuple-element.12, f32[8,96,4,96,1]{3,1,4,2,0:T(8,128)S(1)} %copy-done.4), kind=kLoop, calls=%fused_computation.4 | loop fusion | flops 294912 | bytes 3538944 | tf_op jit(solution)/shard_map/sub | solution.py:282
  58.6 1.9 %copy.13 = f32[4,8,96,96]{3,2,1,0:T(8,128)S(1)} copy(f32[4,8,96,96]{2,3,0,1:T(8,128)} %bitcast_subtract_fusion) | data formatting | bytes 2359296 | tf_op jit(solution)/shard_map/sub | solution.py:282
  60.5 1.9 %reshape.19.p_ref = f32[4,8,9216]{2,1,0:T(8,128)} reshape(f32[4,8,96,96]{3,2,1,0:T(8,128)S(1)} %copy.13) | data formatting | bytes 2359296 | tf_op jit(solution)/shard_map/reshape | solution.py:284
  62.4 2.1 %reshape.18.s_ref = f32[8,4,9216]{2,1,0:T(4,128)} reshape(f32[8,4,96,96]{3,2,1,0:T(8,128)S(1)} %get-tuple-element.11) | data formatting | bytes 2359296 | tf_op jit(solution)/shard_map/reshape | solution.py:283
  64.6 32.9 %exchange.1 = f32[128,2304]{1,0:T(8,128)} custom-call(f32[8,4,9216]{2,1,0:T(4,128)} %reshape.18.s_ref, f32[4,8,9216]{2,1,0:T(8,128)} %reshape.19.p_ref, bf16[256,4608]{1,0:T(8,128)(2,1)} %copy-done, bf16[4608,2304]{1,0:T(8,128)(2,1)} %v_ref.1, f32[128,2304]{1,0:T(8,128)} %copy-done.2, bf16[128,2304]{1,0:T(8,128)(2,1)} %oovv_ref.3, f32[128,2304]{1,0:T(8,128)} %den_ref.1), custom_call_target="tpu_custom_call" | custom-call | tf_op jit(solution)/shard_map/exchange/pallas_call | solution.py:255
  97.5 2.4 %copy.33 = f32[128,2304]{1,0:T(8,128)} copy(f32[128,2304]{1,0:T(8,128)} %exchange.1) | data formatting | bytes 2359296
Async XLA Ops:
  0.0 1.4 %copy-start.3 = (bf16[256,256]{1,0:T(8,128)(2,1)S(1)}, bf16[256,256]{1,0:T(8,128)(2,1)}, u32[]{:S(2)}) copy-start(bf16[256,256]{1,0:T(8,128)(2,1)} %oooo_ref.1) | copy-start | bytes 393220
  0.0 1.5 %copy-start.1 = (bf16[128,2304]{1,0:T(8,128)(2,1)S(1)}, bf16[128,2304]{1,0:T(8,128)(2,1)}, u32[]{:S(2)}) copy-start(bf16[128,2304]{1,0:T(8,128)(2,1)} %oovv_ref.3) | copy-start | bytes 1769476
  31.2 1.5 %copy-start = (bf16[256,4608]{1,0:T(8,128)(2,1)}, bf16[256,4608]{1,0:T(8,128)(2,1)S(1)}, u32[]{:S(2)}) copy-start(bf16[256,4608]{1,0:T(8,128)(2,1)S(1)} %get-tuple-element.9.t_ref) | copy-start | bytes 7077892
  32.6 1.1 %copy-start.2 = (f32[128,2304]{1,0:T(8,128)}, f32[128,2304]{1,0:T(8,128)S(1)}, u32[]{:S(2)}) copy-start(f32[128,2304]{1,0:T(8,128)S(1)} %get-tuple-element.10.hole_ref) | copy-start | bytes 3538948
  33.7 4.1 %copy-start.5 = (bf16[1536,384]{1,0:T(8,128)(2,1)S(1)}, bf16[1536,384]{1,0:T(8,128)(2,1)}, u32[]{:S(2)}) copy-start(bf16[1536,384]{1,0:T(8,128)(2,1)} %param.12) | copy-start | bytes 3538948
  49.1 4.4 %copy-start.4 = (f32[8,96,4,96,1]{3,1,4,2,0:T(8,128)S(1)}, f32[8,96,4,96,1]{3,1,4,2,0:T(8,128)}, u32[]{:S(2)}) copy-start(f32[8,96,4,96,1]{3,1,4,2,0:T(8,128)} %fusion.2) | copy-start | bytes 3538948

commit v2 on v0

v2 whole, which is shorter than its diff:
```python
import jax
import jax.numpy as jnp
from jax import lax
from jax.experimental import pallas as pl
from jax.experimental.pallas import tpu as pltpu
from jax.sharding import PartitionSpec as P

MESH = pl.DeviceIdType.MESH
F32 = jnp.float32
BF16 = jnp.bfloat16
NT = (((1,), (1,)), ((), ()))
TN = (((0,), (0,)), ((), ()))

OCC = 16
VIRT = 96
LANE = 128
PITCH = 104
STEP = 256


def _dev(c, r):
    return {"col": c, "row": r}


def _rcopy(src, dst, ssem, rsem, dev):
    return pltpu.make_async_remote_copy(src, dst, ssem, rsem, device_id=dev, device_id_type=MESH)


def sweep_kernel(t_hbm, oovv_hbm, v_hbm, oooo_hbm, wd_hbm, wx_hbm, out_ref,
                 t32, oovv, oooo, wd, wx, tg, xp, xr, mfull, hole, t4, wd4, wxt, ubuf, vbuf_s, s4, st4,
                 smsg, pmsg, srecv, precv, vv, tl, mine, theirs, part,
                 lsem, gs, gr, xs, xrs, ms, mrs, ss, srs, ps, prs, vsem, rs, rrs):
    r, c = lax.axis_index("row"), lax.axis_index("col")
    x, y = c % 2, c // 2
    o = 1 - r
    nx, ny, dg = y * 2 + (1 - x), (1 - y) * 2 + x, (1 - y) * 2 + (1 - x)
    n, w = t32.shape
    h = w // 2
    h0, h1 = pl.ds(0, h), pl.ds(h, h)
    rows = pl.ds(pl.multiple_of(r * n, n), n)
    orows = pl.ds(pl.multiple_of(o * n, n), n)

    loads = [pltpu.make_async_copy(a, b, lsem.at[k]) for k, (a, b) in enumerate(
        ((t_hbm, t32), (oovv_hbm, oovv), (oooo_hbm, oooo), (wd_hbm, wd), (wx_hbm, wx)))]
    for cp in loads:
        cp.start()

    def vcopy(s, slot):
        lanes = pl.ds(pl.multiple_of(s * STEP, STEP), STEP)
        return pltpu.make_async_copy(v_hbm.at[:, lanes], vv.at[slot], vsem.at[slot])

    loads[0].wait()
    tg[c, rows, :] = t32[...].astype(BF16)

    sem = pltpu.get_barrier_semaphore()
    for cc, rr in ((nx, r), (ny, r), (dg, r), (c, o), (nx, o), (ny, o), (dg, o)):
        pl.semaphore_signal(sem, inc=1, device_id=_dev(cc, rr), device_id_type=MESH)
    pl.semaphore_wait(sem, 7)

    def tcopy(chip, lanes, k, dev):
        ref = tg.at[chip, rows, lanes]
        return _rcopy(ref, ref, gs.at[k], gr.at[k], dev)

    whole = pl.ds(0, w)
    x0 = tcopy(c, h0, 1, _dev(nx, r))
    y1 = tcopy(c, h1, 2, _dev(ny, r))
    d_own = tcopy(c, whole, 0, _dev(c, o))
    x1 = tcopy(c, h1, 3, _dev(nx, r))
    y0 = tcopy(c, h0, 4, _dev(ny, r))
    x0.start()
    y1.start()
    d_own.start()
    vcopy(0, 0).start()
    vcopy(1, 1).start()

    loads[1].wait()
    loads[2].wait()
    d_own.wait_recv()
    xp[...] = lax.dot_general(oovv[...], tg[c], NT, preferred_element_type=F32)
    q = n // 4
    xcopies = []
    for s, cc in enumerate((nx, ny, dg)):
        cp = _rcopy(xp.at[pl.ds(pl.multiple_of(cc * q, q), q)], xr.at[c], xs.at[s], xrs.at[s], _dev(cc, r))
        cp.start()
        xcopies.append(cp)
    x1.start()
    y0.start()
    xr[c, :, :] = xp[pl.ds(pl.multiple_of(c * q, q), q), :]

    def spread(chip, first, groups):
        @pl.loop(0, n // 16)
        def _(ib):
            for g in range(first, first + groups):
                tile = tg[chip, pl.ds(pl.multiple_of(r * n + ib * 16, 16), 16), g * 384:(g + 1) * 384].astype(F32)
                for e in range(4):
                    slab = tile[:, e * VIRT:(e + 1) * VIRT]
                    slab = jnp.concatenate([slab, jnp.zeros((16, LANE - VIRT), F32)], axis=1)
                    for half in range(2):
                        start = (ib * 16 + half * 8) * PITCH + chip * 24 + g * 4 + e
                        t4[pl.ds(start, 8, stride=PITCH), :] = slab[half * 8:half * 8 + 8]

    spread(c, 0, 6)

    loads[3].wait()
    loads[4].wait()
    zrow = jnp.zeros((LANE - VIRT, 4 * LANE), BF16)

    @pl.loop(0, OCC)
    def _(k):
        blk = wd[pl.ds(pl.multiple_of(k * VIRT, 16), VIRT), :].astype(F32)
        parts = []
        for j in range(4):
            parts += [blk[:, j * VIRT:(j + 1) * VIRT], jnp.zeros((VIRT, LANE - VIRT), F32)]
        wd4[pl.ds(pl.multiple_of(k * LANE, LANE), VIRT), :] = jnp.concatenate(parts, axis=1).astype(BF16)
        wd4[pl.ds(pl.multiple_of(k * LANE + VIRT, 32), LANE - VIRT), :] = zrow

    for b in range(3):
        wxt[b * LANE:(b + 1) * LANE, :] = wx[:, b * LANE:(b + 1) * LANE].T

    for cp in xcopies:
        cp.wait_recv()
    xsum = (xr[0] + xr[1]) + (xr[2] + xr[3])
    krows = pl.ds(pl.multiple_of(r * n + c * q, q), q)
    mfull[krows, :] = (oooo[krows, :].astype(F32) + 0.5 * xsum).astype(BF16)
    mcopies = []
    for s, (cc, rr) in enumerate(((nx, r), (ny, r), (dg, r), (c, o), (nx, o), (ny, o), (dg, o))):
        cp = _rcopy(mfull.at[krows], mfull.at[krows], ms.at[s], mrs.at[s], _dev(cc, rr))
        cp.start()
        mcopies.append(cp)

    x0.wait_recv()
    f0 = tcopy(nx, h0, 5, _dev(ny, r))
    f0.start()
    y1.wait_recv()
    f1 = tcopy(ny, h1, 6, _dev(nx, r))
    f1.start()
    spread(nx, 0, 3)
    spread(ny, 3, 3)
    x1.wait_recv()
    d_x = tcopy(nx, whole, 7, _dev(c, o))
    d_x.start()
    y0.wait_recv()
    d_y = tcopy(ny, whole, 8, _dev(c, o))
    d_y.start()
    spread(nx, 3, 3)
    spread(ny, 0, 3)

    for cp in mcopies:
        cp.wait_recv()
    m_mine = mfull[:, rows]

    @pl.loop(0, w // STEP)
    def _(s):
        lanes = pl.ds(pl.multiple_of(s * STEP, STEP), STEP)
        hole[:, lanes] = lax.dot_general(m_mine, tg[c, :, lanes], TN, preferred_element_type=F32)

    f0.wait_recv()
    f1.wait_recv()
    d_d = tcopy(dg, whole, 9, _dev(c, o))
    d_d.start()
    spread(dg, 0, 6)

    @pl.loop(0, OCC // 2)
    def _(k2):
        halves = []
        for e in range(2):
            halves.append(jnp.concatenate(
                [t4[pl.ds(pl.multiple_of((i * OCC + 2 * k2 + e) * PITCH, 8), VIRT), :] for i in range(8)], axis=0))
        lhs = jnp.concatenate(halves, axis=1).astype(BF16)
        prod = jnp.dot(lhs, wd4[pl.ds(pl.multiple_of(k2 * 256, 256), 256), :], preferred_element_type=F32)

        @pl.when(k2 == 0)
        def _():
            ubuf[...] = prod

        @pl.when(k2 > 0)
        def _():
            ubuf[...] += prod

    @pl.loop(0, 4)
    def _(i2):
        halves = []
        for e in range(2):
            halves.append(jnp.concatenate(
                [t4[pl.ds(pl.multiple_of(((2 * i2 + e) * OCC + k) * PITCH, 8), VIRT), :] for k in range(OCC)], axis=0))
        rhs = jnp.concatenate(halves, axis=1).astype(BF16)
        vbuf_s[i2, :, :] = jnp.dot(wxt[...], rhs, preferred_element_type=F32)

    own = c // 2
    half = c % 2

    def put(src, chip, dst):
        for g in range(6):
            vals = [src[pl.ds(chip * 24 + g * 4 + e, 8, stride=PITCH), :][:, :VIRT] for e in range(4)]
            dst[:, g * 384:(g + 1) * 384] = jnp.concatenate(vals, axis=1)

    dests = (dg, nx, ny)

    def scopy(j, s):
        return _rcopy(smsg.at[s, j], srecv.at[c, j], ss.at[s, j], srs.at[c, j], _dev(dests[s], r))

    def pcopy(j, s):
        chip = (dg, nx, ny, c)[s]
        return _rcopy(pmsg.at[s, j], precv.at[half, r, j], ps.at[s, j], prs.at[half, r, j], _dev(chip, own))

    @pl.loop(0, 4)
    def _(j):
        for i in range(8):
            blk = (ubuf[i * VIRT:(i + 1) * VIRT, pl.ds(pl.multiple_of(j * LANE, LANE), LANE)]
                   - vbuf_s[i // 2, pl.ds(pl.multiple_of(j * VIRT, 8), VIRT), (i % 2) * LANE:(i % 2 + 1) * LANE])
            s4[i * PITCH:i * PITCH + VIRT, :] = blk
            st4[i * PITCH:i * PITCH + VIRT, :VIRT] = blk.T[:VIRT, :]
        for s in range(3):
            put(s4, dests[s], smsg.at[s, j])
            scopy(j, s).start()
            put(st4, dests[s], pmsg.at[s, j])
            pcopy(j, s).start()
        put(s4, c, srecv.at[c, j])

        @pl.when(own == r)
        def _():
            put(st4, c, precv.at[half, r, j])

        @pl.when(own != r)
        def _():
            put(st4, c, pmsg.at[3, j])
            pcopy(j, 3).start()

    d_x.wait_recv()
    d_y.wait_recv()
    d_d.wait_recv()

    def ladder_copy(s):
        lanes = pl.ds(pl.multiple_of(s * STEP, STEP), STEP)
        return _rcopy(part.at[s], theirs.at[:, lanes], rs.at[s], rrs.at[s], _dev(c, o))

    @pl.loop(0, w // STEP)
    def _(s):
        slot = s % 3

        @pl.when(s + 2 < w // STEP)
        def _():
            vcopy(s + 2, (s + 2) % 3).start()

        vcopy(s, slot).wait()
        lanes = pl.ds(pl.multiple_of(s * STEP, STEP), STEP)
        va, vb = vv.at[slot, pl.ds(0, w)], vv.at[slot, pl.ds(w, w)]
        part[s, :, :] = (jnp.dot(tg[2 * r, orows, :], va[...], preferred_element_type=F32)
                         + jnp.dot(tg[2 * r + 1, orows, :], vb[...], preferred_element_type=F32))
        ladder_copy(s).start()
        mine[:, lanes] = (jnp.dot(tg[2 * r, rows, :], va[...], preferred_element_type=F32)
                          + jnp.dot(tg[2 * r + 1, rows, :], vb[...], preferred_element_type=F32))

    @pl.loop(0, w // STEP)
    def _(s):
        ladder_copy(s).wait()

    for cp in (d_own, x0, y1, x1, y0, f0, f1, d_x, d_y, d_d, *xcopies, *mcopies):
        cp.wait_send()

    @pl.loop(0, 8)
    def _(i):
        line = pl.ds(pl.multiple_of(i * 16, 16), 16)
        out_ref[line, :] = oovv[line, :].astype(F32) + (mine[line, :] + theirs[line, :] + hole[line, :])

    for s in range(3):
        @pl.loop(0, 4)
        def _(j):
            scopy(j, s).wait_send()
            pcopy(j, s).wait_send()

    @pl.when(own != r)
    def _():
        @pl.loop(0, 4)
        def _(j):
            pcopy(j, 3).wait_send()

    def landed(dst, sem):
        return pltpu.make_async_copy(dst, dst, sem)

    for a, chip in enumerate((nx, ny, dg)):
        @pl.loop(0, 4)
        def _(j):
            landed(srecv.at[chip, j], srs.at[chip, j]).wait()

    for a in range(2):
        for b in range(2):
            here = jnp.logical_and(c == 2 * r + a, r == b)

            @pl.when(jnp.logical_not(here))
            def _():
                @pl.loop(0, 4)
                def _(j):
                    landed(precv.at[a, b, j], prs.at[a, b, j]).wait()

    @pl.loop(0, 8)
    def _(i):
        for jh in range(2):
            line = pl.ds(pl.multiple_of(i * 16 + jh * 8, 8), 8)
            sv = jnp.concatenate([srecv.at[2 * jh + e // 4, e % 4][pl.ds(i, 1), :] for e in range(8)], axis=0)
            out_ref[line, :] = out_ref[line, :] + (sv + precv[i // 4, jh, i % 4])


ANY = pl.BlockSpec(memory_space=pl.ANY)
DMA = pltpu.SemaphoreType.DMA


def sweep(t, oovv, vvvv, oooo, wd, wx):
    n, w = t.shape
    depth = vvvv.shape[0]
    V = pltpu.VMEM
    return pl.pallas_call(
        sweep_kernel,
        out_shape=jax.ShapeDtypeStruct((n, w), F32),
        in_specs=[ANY] * 6,
        out_specs=pl.BlockSpec(memory_space=pltpu.VMEM),
        scratch_shapes=[
            V((n, w), F32), V((n, w), BF16), V(oooo.shape, BF16), V(wd.shape, BF16), V(wx.shape, BF16),
            V((4, 2 * n, w), BF16),
            V((n, 2 * n), F32), V((4, n // 4, 2 * n), F32), V((2 * n, 2 * n), BF16), V((n, w), F32),
            V((n * PITCH, LANE), F32), V((OCC * LANE, 4 * LANE), BF16), V((wx.shape[1], wx.shape[0]), BF16),
            V((8 * VIRT, 4 * LANE), F32), V((4, 4 * VIRT, 2 * LANE), F32),
            V((8 * PITCH, LANE), F32), V((8 * PITCH, LANE), F32),
            V((3, 4, 8, w), F32), V((4, 4, 8, w), F32), V((4, 4, 8, w), F32), V((2, 2, 4, 8, w), F32),
            V((3, depth, STEP), BF16), V((8, LANE), BF16), V((n, w), F32), V((n, w), F32), V((w // STEP, n, STEP), F32),
            DMA((5,)), DMA((10,)), DMA((10,)), DMA((3,)), DMA((3,)), DMA((7,)), DMA((7,)),
            DMA((3, 4)), DMA((4, 4)), DMA((4, 4)), DMA((2, 2, 4)), DMA((3,)), DMA((w // STEP,)), DMA((w // STEP,)),
        ],
        compiler_params=pltpu.CompilerParams(collective_id=0, has_side_effects=True, vmem_limit_bytes=60 << 20),
        name="sweep",
    )(t, oovv, vvvv, oooo, wd, wx)


def solution(mesh):
    def local_sweep(t_blk, d_blk, oovv_blk, vvvv_blk, oooo_full, wd_blk, wx_blk):
        return sweep(t_blk, oovv_blk, vvvv_blk, oooo_full, wd_blk, wx_blk) / d_blk

    amp = P("row", "col")
    wide = P(None, "col")
    return jax.shard_map(local_sweep, mesh=mesh, in_specs=(amp, amp, amp, amp, P(), wide, wide), out_specs=amp, check_vma=False)
```

time: 231 us -> 68.9 us (0.30)
  waiting for transfers between devices: 72 us -> 0 us
  Pallas kernels: 0 us -> 66.3 us
  local copies, waits for them, and re-layouts: 56.1 us -> 0.01 us
  blocking collectives: 53.6 us -> 0 us
  matrix products: 25.7 us -> 0 us
  between operations: 13.2 us -> 0.02 us
  other arithmetic: 9.56 us -> 2.44 us
    pallas_call x0 -> x1, Pallas kernels: none -> 66.3 us  [sweep(): pl.pallas_call(sweep_kernel, out_shape=jax.ShapeDtypeStruct((n, w), F32),...]
    all_to_all x4 -> x0, blocking collectives: 53.6 us -> none  [the longest x1 22.8 us: local_sweep(): ph_back = lax.all_to_all(direct_term - exch_term, 'col', 2, 1, tiled=True)]
    all_gather x2 -> x0, waiting for transfers between devices: 39.4 us -> none  [the longest x1 30.5 us: local_sweep(): t_rows = lax.all_gather(t_half, 'col', axis=1, tiled=True)]
    psum x1 -> x0, waiting for transfers between devices: 31.8 us -> none  [local_sweep(): x_rows = lax.psum(x_part, 'col')]
    dot_general x5 -> x0, matrix products: 25.7 us -> none  [the longest x1 14.6 us: local_sweep(): jnp.dot(t_ladder, vvvv_blk, preferred_element_type=jnp.float32)]
    all_to_all x8 -> x0, local copies, waits for them, and re-layouts: 24.2 us -> none  [the longest x3 15.8 us: local_sweep(): swap_both = lax.all_to_all(swap_row, 'col', 3, 2, tiled=True)]
    unnamed x17 -> x2, local copies, waits for them, and re-layouts: 17.5 us -> 0.01 us
    reshape x4 -> x0, local copies, waits for them, and re-layouts: 9.12 us -> none  [the longest x1 4.47 us: local_sweep(): t_four = t_rows.reshape(occ_row, n_occ, n_virt, n_virt)]
  transfers between devices with their start and end apart: 4 -> 0, of which waited for: 3 -> 0; matrix products, arithmetic and copies ran while one was open for 26% -> 0% of each run, Pallas kernels for 0% -> 0%
where the time goes in v2:
time: 68.9 us; the launch traced here: 68.7 us
  Pallas kernels  66.3 us (96%)
  other arithmetic  2.44 us (4%)
    pallas_call x1, Pallas kernels, sweep(): pl.pallas_call(sweep_kernel, out_shape=jax.ShapeDtypeStruct((n, w), F32),...  66.3 us
    div x1, other arithmetic, local_sweep(): return sweep(t_blk, oovv_blk, vvvv_blk, oooo_full, wd_blk, wx_blk) / d_blk  2.44 us

profile of v2, /device:TPU:0, one launch (start us, length us, event | category | flops | bytes accessed | tf_op | source)
XLA Modules:
  0.0 68.7 jit_solution(10660825224473825014)
XLA Ops:
  0.0 0.0 copy-start
  0.0 66.3 %sweep.1 = f32[128,2304]{1,0:T(8,128)} custom-call(f32[128,2304]{1,0:T(8,128)} %t_hbm.1, bf16[128,2304]{1,0:T(8,128)(2,1)} %oovv_hbm.1, bf16[4608,2304]{1,0:T(8,128)(2,1)} %v_hbm.1, bf16[256,256]{1,0:T(8,128)(2,1)} %oooo_hbm.1, bf16[1536,384]{1,0:T(8,128)(2,1)} %wd_hbm.1, bf16[1536,384]{1,0:T(8,128)(2,1)} %wx_hbm.1), custom_call_target="tpu_custom_call" | custom-call | tf_op jit(solution)/shard_map/sweep/pallas_call | solution.py:312
  66.3 0.0 copy-done
  66.3 2.4 %div.3 = f32[128,2304]{1,0:T(8,128)} divide(f32[128,2304]{1,0:T(8,128)} %sweep.1, f32[128,2304]{1,0:T(8,128)S(1)} %copy-done) | non-fusion elementwise | flops 294912 | bytes 3538944 | tf_op jit(solution)/shard_map/div | solution.py:336
Async XLA Ops:
  0.0 66.3 %copy-start = (f32[128,2304]{1,0:T(8,128)S(1)}, f32[128,2304]{1,0:T(8,128)}, u32[]{:S(2)}) copy-start(f32[128,2304]{1,0:T(8,128)} %param.8) | copy-start | bytes 3538948

commit v3 on v2

--- a/solution.py
+++ b/solution.py
@@ -28,7 +28,7 @@
 
 def sweep_kernel(t_hbm, oovv_hbm, v_hbm, oooo_hbm, wd_hbm, wx_hbm, out_ref,
                  t32, oovv, oooo, wd, wx, tg, xp, xr, mfull, hole, t4, wd4, wxt, ubuf, vbuf_s, s4, st4,
-                 smsg, pmsg, srecv, precv, vv, tl, mine, theirs, part,
+                 smsg, pmsg, srecv, precv, vv, theirs, part, wxf,
                  lsem, gs, gr, xs, xrs, ms, mrs, ss, srs, ps, prs, vsem, rs, rrs):
     r, c = lax.axis_index("row"), lax.axis_index("col")
     x, y = c % 2, c // 2
@@ -40,6 +40,9 @@
     rows = pl.ds(pl.multiple_of(r * n, n), n)
     orows = pl.ds(pl.multiple_of(o * n, n), n)
 
+    sem = pltpu.get_barrier_semaphore()
+    for cc, rr in ((nx, r), (ny, r), (dg, r), (c, o), (nx, o), (ny, o), (dg, o)):
+        pl.semaphore_signal(sem, inc=1, device_id=_dev(cc, rr), device_id_type=MESH)
     loads = [pltpu.make_async_copy(a, b, lsem.at[k]) for k, (a, b) in enumerate(
         ((t_hbm, t32), (oovv_hbm, oovv), (oooo_hbm, oooo), (wd_hbm, wd), (wx_hbm, wx)))]
     for cp in loads:
@@ -52,9 +55,6 @@
     loads[0].wait()
     tg[c, rows, :] = t32[...].astype(BF16)
 
-    sem = pltpu.get_barrier_semaphore()
-    for cc, rr in ((nx, r), (ny, r), (dg, r), (c, o), (nx, o), (ny, o), (dg, o)):
-        pl.semaphore_signal(sem, inc=1, device_id=_dev(cc, rr), device_id_type=MESH)
     pl.semaphore_wait(sem, 7)
 
     def tcopy(chip, lanes, k, dev):
@@ -70,22 +70,10 @@
     x0.start()
     y1.start()
     d_own.start()
+    x1.start()
+    y0.start()
     vcopy(0, 0).start()
     vcopy(1, 1).start()
-
-    loads[1].wait()
-    loads[2].wait()
-    d_own.wait_recv()
-    xp[...] = lax.dot_general(oovv[...], tg[c], NT, preferred_element_type=F32)
-    q = n // 4
-    xcopies = []
-    for s, cc in enumerate((nx, ny, dg)):
-        cp = _rcopy(xp.at[pl.ds(pl.multiple_of(cc * q, q), q)], xr.at[c], xs.at[s], xrs.at[s], _dev(cc, r))
-        cp.start()
-        xcopies.append(cp)
-    x1.start()
-    y0.start()
-    xr[c, :, :] = xp[pl.ds(pl.multiple_of(c * q, q), q), :]
 
     def spread(chip, first, groups):
         @pl.loop(0, n // 16)
@@ -113,20 +101,40 @@
             parts += [blk[:, j * VIRT:(j + 1) * VIRT], jnp.zeros((VIRT, LANE - VIRT), F32)]
         wd4[pl.ds(pl.multiple_of(k * LANE, LANE), VIRT), :] = jnp.concatenate(parts, axis=1).astype(BF16)
         wd4[pl.ds(pl.multiple_of(k * LANE + VIRT, 32), LANE - VIRT), :] = zrow
-
-    for b in range(3):
-        wxt[b * LANE:(b + 1) * LANE, :] = wx[:, b * LANE:(b + 1) * LANE].T
-
-    for cp in xcopies:
-        cp.wait_recv()
-    xsum = (xr[0] + xr[1]) + (xr[2] + xr[3])
-    krows = pl.ds(pl.multiple_of(r * n + c * q, q), q)
-    mfull[krows, :] = (oooo[krows, :].astype(F32) + 0.5 * xsum).astype(BF16)
-    mcopies = []
-    for s, (cc, rr) in enumerate(((nx, r), (ny, r), (dg, r), (c, o), (nx, o), (ny, o), (dg, o))):
-        cp = _rcopy(mfull.at[krows], mfull.at[krows], ms.at[s], mrs.at[s], _dev(cc, rr))
-        cp.start()
-        mcopies.append(cp)
+        wxf[pl.ds(pl.multiple_of(k * VIRT, 16), VIRT), :] = wx[pl.ds(pl.multiple_of(k * VIRT, 16), VIRT), :].astype(F32)
+
+    for s, chip in enumerate((c, nx, ny, dg)):
+        for b in range(3):
+            blk = jnp.concatenate(
+                [wxf[pl.ds(pl.multiple_of(k * VIRT + chip * 24, 8), 24), b * LANE:(b + 1) * LANE] for k in range(OCC)],
+                axis=0)
+            wxt[b * LANE:(b + 1) * LANE, s * 384:(s + 1) * 384] = blk.astype(BF16).T
+
+    loads[1].wait()
+    loads[2].wait()
+    d_own.wait_recv()
+    xp[...] = lax.dot_general(oovv[...], tg[c], NT, preferred_element_type=F32)
+
+    def direct(chip):
+        lhs = jnp.concatenate(
+            [jnp.concatenate(
+                [t4[pl.ds(pl.multiple_of((i * OCC + k) * PITCH + chip * 24, 8), 24), :] for i in range(8)], axis=0)
+             for k in range(OCC)], axis=1).astype(BF16)
+        ubuf[chip, :, :] = jnp.dot(lhs, wd4[...], preferred_element_type=F32)
+
+    def exchange(chips, first):
+        @pl.loop(0, 4)
+        def _(i2):
+            halves = []
+            for e in range(2):
+                halves.append(jnp.concatenate(
+                    [t4[pl.ds(pl.multiple_of(((2 * i2 + e) * OCC + k) * PITCH + chip * 24, 8), 24), :]
+                     for chip in chips for k in range(OCC)], axis=0))
+            rhs = jnp.concatenate(halves, axis=1).astype(BF16)
+            prod = jnp.dot(wxt[:, first * 384:(first + len(chips)) * 384], rhs, preferred_element_type=F32)
+            vbuf_s[i2, :, :] = prod if first == 0 else vbuf_s[i2, :, :] + prod
+
+    direct(c)
 
     x0.wait_recv()
     f0 = tcopy(nx, h0, 5, _dev(ny, r))
@@ -134,6 +142,13 @@
     y1.wait_recv()
     f1 = tcopy(ny, h1, 6, _dev(nx, r))
     f1.start()
+    q = n // 4
+    xcopies = []
+    for s, cc in enumerate((nx, ny, dg)):
+        cp = _rcopy(xp.at[pl.ds(pl.multiple_of(cc * q, q), q)], xr.at[c], xs.at[s], xrs.at[s], _dev(cc, r))
+        cp.start()
+        xcopies.append(cp)
+    xr[c, :, :] = xp[pl.ds(pl.multiple_of(c * q, q), q), :]
     spread(nx, 0, 3)
     spread(ny, 3, 3)
     x1.wait_recv()
@@ -144,47 +159,17 @@
     d_y.start()
     spread(nx, 3, 3)
     spread(ny, 0, 3)
-
-    for cp in mcopies:
-        cp.wait_recv()
-    m_mine = mfull[:, rows]
-
-    @pl.loop(0, w // STEP)
-    def _(s):
-        lanes = pl.ds(pl.multiple_of(s * STEP, STEP), STEP)
-        hole[:, lanes] = lax.dot_general(m_mine, tg[c, :, lanes], TN, preferred_element_type=F32)
+    direct(nx)
+    direct(ny)
+    exchange((c, nx, ny), 0)
 
     f0.wait_recv()
     f1.wait_recv()
     d_d = tcopy(dg, whole, 9, _dev(c, o))
     d_d.start()
     spread(dg, 0, 6)
-
-    @pl.loop(0, OCC // 2)
-    def _(k2):
-        halves = []
-        for e in range(2):
-            halves.append(jnp.concatenate(
-                [t4[pl.ds(pl.multiple_of((i * OCC + 2 * k2 + e) * PITCH, 8), VIRT), :] for i in range(8)], axis=0))
-        lhs = jnp.concatenate(halves, axis=1).astype(BF16)
-        prod = jnp.dot(lhs, wd4[pl.ds(pl.multiple_of(k2 * 256, 256), 256), :], preferred_element_type=F32)
-
-        @pl.when(k2 == 0)
-        def _():
-            ubuf[...] = prod
-
-        @pl.when(k2 > 0)
-        def _():
-            ubuf[...] += prod
-
-    @pl.loop(0, 4)
-    def _(i2):
-        halves = []
-        for e in range(2):
-            halves.append(jnp.concatenate(
-                [t4[pl.ds(pl.multiple_of(((2 * i2 + e) * OCC + k) * PITCH, 8), VIRT), :] for k in range(OCC)], axis=0))
-        rhs = jnp.concatenate(halves, axis=1).astype(BF16)
-        vbuf_s[i2, :, :] = jnp.dot(wxt[...], rhs, preferred_element_type=F32)
+    direct(dg)
+    exchange((dg,), 3)
 
     own = c // 2
     half = c % 2
@@ -206,13 +191,17 @@
     @pl.loop(0, 4)
     def _(j):
         for i in range(8):
-            blk = (ubuf[i * VIRT:(i + 1) * VIRT, pl.ds(pl.multiple_of(j * LANE, LANE), LANE)]
-                   - vbuf_s[i // 2, pl.ds(pl.multiple_of(j * VIRT, 8), VIRT), (i % 2) * LANE:(i % 2 + 1) * LANE])
-            s4[i * PITCH:i * PITCH + VIRT, :] = blk
-            st4[i * PITCH:i * PITCH + VIRT, :VIRT] = blk.T[:VIRT, :]
+            blk = jnp.concatenate(
+                [ubuf[chip, i * 24:(i + 1) * 24, pl.ds(pl.multiple_of(j * LANE, LANE), LANE)] for chip in range(4)],
+                axis=0)
+            s4[i * PITCH:i * PITCH + VIRT, :] = blk - vbuf_s[
+                i // 2, pl.ds(pl.multiple_of(j * VIRT, 8), VIRT), (i % 2) * LANE:(i % 2 + 1) * LANE]
         for s in range(3):
             put(s4, dests[s], smsg.at[s, j])
             scopy(j, s).start()
+        for i in range(8):
+            st4[i * PITCH:i * PITCH + VIRT, :VIRT] = s4[i * PITCH:i * PITCH + VIRT, :].T[:VIRT, :]
+        for s in range(3):
             put(st4, dests[s], pmsg.at[s, j])
             pcopy(j, s).start()
         put(s4, c, srecv.at[c, j])
@@ -226,13 +215,25 @@
             put(st4, c, pmsg.at[3, j])
             pcopy(j, 3).start()
 
+    for cp in xcopies:
+        cp.wait_recv()
+    xsum = (xr[0] + xr[1]) + (xr[2] + xr[3])
+    krows = pl.ds(pl.multiple_of(r * n + c * q, q), q)
+    mfull[krows, :] = (oooo[krows, :].astype(F32) + 0.5 * xsum).astype(BF16)
+    mcopies = []
+    for s, (cc, rr) in enumerate(((nx, r), (ny, r), (dg, r), (c, o), (nx, o), (ny, o), (dg, o))):
+        part_m = mfull.at[krows, pl.ds(pl.multiple_of(rr * n, n), n)]
+        cp = _rcopy(part_m, part_m, ms.at[s], mrs.at[s], _dev(cc, rr))
+        cp.start()
+        mcopies.append(cp)
+
     d_x.wait_recv()
     d_y.wait_recv()
     d_d.wait_recv()
 
     def ladder_copy(s):
         lanes = pl.ds(pl.multiple_of(s * STEP, STEP), STEP)
-        return _rcopy(part.at[s], theirs.at[:, lanes], rs.at[s], rrs.at[s], _dev(c, o))
+        return _rcopy(part.at[s, orows], theirs.at[:, lanes], rs.at[s], rrs.at[s], _dev(c, o))
 
     @pl.loop(0, w // STEP)
     def _(s):
@@ -243,13 +244,10 @@
             vcopy(s + 2, (s + 2) % 3).start()
 
         vcopy(s, slot).wait()
-        lanes = pl.ds(pl.multiple_of(s * STEP, STEP), STEP)
         va, vb = vv.at[slot, pl.ds(0, w)], vv.at[slot, pl.ds(w, w)]
-        part[s, :, :] = (jnp.dot(tg[2 * r, orows, :], va[...], preferred_element_type=F32)
-                         + jnp.dot(tg[2 * r + 1, orows, :], vb[...], preferred_element_type=F32))
+        part[s, :, :] = (jnp.dot(tg[2 * r], va[...], preferred_element_type=F32)
+                         + jnp.dot(tg[2 * r + 1], vb[...], preferred_element_type=F32))
         ladder_copy(s).start()
-        mine[:, lanes] = (jnp.dot(tg[2 * r, rows, :], va[...], preferred_element_type=F32)
-                          + jnp.dot(tg[2 * r + 1, rows, :], vb[...], preferred_element_type=F32))
 
     @pl.loop(0, w // STEP)
     def _(s):
@@ -258,10 +256,21 @@
     for cp in (d_own, x0, y1, x1, y0, f0, f1, d_x, d_y, d_d, *xcopies, *mcopies):
         cp.wait_send()
 
+    for cp in mcopies:
+        cp.wait_recv()
+    m_mine = mfull[:, rows]
+
+    @pl.loop(0, w // STEP)
+    def _(s):
+        lanes = pl.ds(pl.multiple_of(s * STEP, STEP), STEP)
+        hole[:, lanes] = lax.dot_general(m_mine, tg[c, :, lanes], TN, preferred_element_type=F32)
+
     @pl.loop(0, 8)
     def _(i):
         line = pl.ds(pl.multiple_of(i * 16, 16), 16)
-        out_ref[line, :] = oovv[line, :].astype(F32) + (mine[line, :] + theirs[line, :] + hole[line, :])
+        line_r = pl.ds(pl.multiple_of(r * n + i * 16, 16), 16)
+        mine = jnp.concatenate([part[s, line_r, :] for s in range(w // STEP)], axis=1)
+        out_ref[line, :] = oovv[line, :].astype(F32) + (mine + theirs[line, :] + hole[line, :])
 
     for s in range(3):
         @pl.loop(0, 4)
@@ -319,10 +328,10 @@
             V((4, 2 * n, w), BF16),
             V((n, 2 * n), F32), V((4, n // 4, 2 * n), F32), V((2 * n, 2 * n), BF16), V((n, w), F32),
             V((n * PITCH, LANE), F32), V((OCC * LANE, 4 * LANE), BF16), V((wx.shape[1], wx.shape[0]), BF16),
-            V((8 * VIRT, 4 * LANE), F32), V((4, 4 * VIRT, 2 * LANE), F32),
+            V((4, 2 * VIRT, 4 * LANE), F32), V((4, 4 * VIRT, 2 * LANE), F32),
             V((8 * PITCH, LANE), F32), V((8 * PITCH, LANE), F32),
             V((3, 4, 8, w), F32), V((4, 4, 8, w), F32), V((4, 4, 8, w), F32), V((2, 2, 4, 8, w), F32),
-            V((3, depth, STEP), BF16), V((8, LANE), BF16), V((n, w), F32), V((n, w), F32), V((w // STEP, n, STEP), F32),
+            V((3, depth, STEP), BF16), V((n, w), F32), V((w // STEP, 2 * n, STEP), F32), V(wx.shape, F32),
             DMA((5,)), DMA((10,)), DMA((10,)), DMA((3,)), DMA((3,)), DMA((7,)), DMA((7,)),
             DMA((3, 4)), DMA((4, 4)), DMA((4, 4)), DMA((2, 2, 4)), DMA((3,)), DMA((w // STEP,)), DMA((w // STEP,)),
         ],

time: 68.9 us -> 63.1 us (0.916)
  Pallas kernels: 66.3 us -> 60.5 us
    pallas_call x1, Pallas kernels: 66.3 us -> 60.5 us  [sweep(): pl.pallas_call(sweep_kernel, out_shape=jax.ShapeDtypeStruct((n, w), F32),...]
where the time goes in v3:
time: 63.1 us; the launch traced here: 63 us
  Pallas kernels  60.5 us (96%)
  other arithmetic  2.44 us (4%)
    pallas_call x1, Pallas kernels, sweep(): pl.pallas_call(sweep_kernel, out_shape=jax.ShapeDtypeStruct((n, w), F32),...  60.5 us
    div x1, other arithmetic, local_sweep(): return sweep(t_blk, oovv_blk, vvvv_blk, oooo_full, wd_blk, wx_blk) / d_blk  2.44 us

profile of v3, /device:TPU:0, one launch (start us, length us, event | category | flops | bytes accessed | tf_op | source)
XLA Modules:
  0.0 63.0 jit_solution(14117889317314553580)
XLA Ops:
  0.0 0.0 copy-start
  0.0 60.5 %sweep.1 = f32[128,2304]{1,0:T(8,128)} custom-call(f32[128,2304]{1,0:T(8,128)} %t_hbm.1, bf16[128,2304]{1,0:T(8,128)(2,1)} %oovv_hbm.1, bf16[4608,2304]{1,0:T(8,128)(2,1)} %v_hbm.1, bf16[256,256]{1,0:T(8,128)(2,1)} %oooo_hbm.1, bf16[1536,384]{1,0:T(8,128)(2,1)} %wd_hbm.1, bf16[1536,384]{1,0:T(8,128)(2,1)} %wx_hbm.1), custom_call_target="tpu_custom_call" | custom-call | tf_op jit(solution)/shard_map/sweep/pallas_call | solution.py:321
  60.5 0.0 copy-done
  60.5 2.4 %div.3 = f32[128,2304]{1,0:T(8,128)} divide(f32[128,2304]{1,0:T(8,128)} %sweep.1, f32[128,2304]{1,0:T(8,128)S(1)} %copy-done) | non-fusion elementwise | flops 294912 | bytes 3538944 | tf_op jit(solution)/shard_map/div | solution.py:345
Async XLA Ops:
  0.0 60.5 %copy-start = (f32[128,2304]{1,0:T(8,128)S(1)}, f32[128,2304]{1,0:T(8,128)}, u32[]{:S(2)}) copy-start(f32[128,2304]{1,0:T(8,128)} %param.8) | copy-start | bytes 3538948

commit v4 on v3

--- a/solution.py
+++ b/solution.py
@@ -29,7 +29,7 @@
 def sweep_kernel(t_hbm, oovv_hbm, v_hbm, oooo_hbm, wd_hbm, wx_hbm, out_ref,
                  t32, oovv, oooo, wd, wx, tg, xp, xr, mfull, hole, t4, wd4, wxt, ubuf, vbuf_s, s4, st4,
                  smsg, pmsg, srecv, precv, vv, theirs, part, wxf,
-                 lsem, gs, gr, xs, xrs, ms, mrs, ss, srs, ps, prs, vsem, rs, rrs):
+                 lsem, gs, gr, fs, fr, xs, xrs, ms, mrs, ss, srs, ps, prs, vsem, rs, rrs):
     r, c = lax.axis_index("row"), lax.axis_index("col")
     x, y = c % 2, c // 2
     o = 1 - r
@@ -60,6 +60,10 @@
     def tcopy(chip, lanes, k, dev):
         ref = tg.at[chip, rows, lanes]
         return _rcopy(ref, ref, gs.at[k], gr.at[k], dev)
+
+    def fcopy(chip, lanes, k, p, dev):
+        ref = tg.at[chip, pl.ds(pl.multiple_of(r * n + p * 32, 32), 32), lanes]
+        return _rcopy(ref, ref, fs.at[k, p], fr.at[k, p], dev)
 
     whole = pl.ds(0, w)
     x0 = tcopy(c, h0, 1, _dev(nx, r))
@@ -75,17 +79,20 @@
     vcopy(0, 0).start()
     vcopy(1, 1).start()
 
+    def spread_rows(chip, ib, first, groups):
+        for g in range(first, first + groups):
+            tile = tg[chip, pl.ds(pl.multiple_of(r * n + ib * 16, 16), 16), g * 384:(g + 1) * 384].astype(F32)
+            for e in range(4):
+                slab = tile[:, e * VIRT:(e + 1) * VIRT]
+                slab = jnp.concatenate([slab, jnp.zeros((16, LANE - VIRT), F32)], axis=1)
+                for half in range(2):
+                    start = (ib * 16 + half * 8) * PITCH + chip * 24 + g * 4 + e
+                    t4[pl.ds(start, 8, stride=PITCH), :] = slab[half * 8:half * 8 + 8]
+
     def spread(chip, first, groups):
         @pl.loop(0, n // 16)
         def _(ib):
-            for g in range(first, first + groups):
-                tile = tg[chip, pl.ds(pl.multiple_of(r * n + ib * 16, 16), 16), g * 384:(g + 1) * 384].astype(F32)
-                for e in range(4):
-                    slab = tile[:, e * VIRT:(e + 1) * VIRT]
-                    slab = jnp.concatenate([slab, jnp.zeros((16, LANE - VIRT), F32)], axis=1)
-                    for half in range(2):
-                        start = (ib * 16 + half * 8) * PITCH + chip * 24 + g * 4 + e
-                        t4[pl.ds(start, 8, stride=PITCH), :] = slab[half * 8:half * 8 + 8]
+            spread_rows(chip, ib, first, groups)
 
     spread(c, 0, 6)
 
@@ -115,33 +122,40 @@
     d_own.wait_recv()
     xp[...] = lax.dot_general(oovv[...], tg[c], NT, preferred_element_type=F32)
 
-    def direct(chip):
+    def direct_rows(chip, i0, count):
         lhs = jnp.concatenate(
             [jnp.concatenate(
-                [t4[pl.ds(pl.multiple_of((i * OCC + k) * PITCH + chip * 24, 8), 24), :] for i in range(8)], axis=0)
+                [t4[pl.ds(pl.multiple_of(((i0 + i) * OCC + k) * PITCH + chip * 24, 8), 24), :] for i in range(count)],
+                axis=0)
              for k in range(OCC)], axis=1).astype(BF16)
-        ubuf[chip, :, :] = jnp.dot(lhs, wd4[...], preferred_element_type=F32)
+        return jnp.dot(lhs, wd4[...], preferred_element_type=F32)
+
+    def direct(chip):
+        ubuf[chip, :, :] = direct_rows(chip, 0, 8)
+
+    def exchange_pair(chips, first, i2):
+        halves = []
+        for e in range(2):
+            halves.append(jnp.concatenate(
+                [t4[pl.ds(pl.multiple_of(((2 * i2 + e) * OCC + k) * PITCH + chip * 24, 8), 24), :]
+                 for chip in chips for k in range(OCC)], axis=0))
+        rhs = jnp.concatenate(halves, axis=1).astype(BF16)
+        prod = jnp.dot(wxt[:, first * 384:(first + len(chips)) * 384], rhs, preferred_element_type=F32)
+        vbuf_s[i2, :, :] = prod if first == 0 else vbuf_s[i2, :, :] + prod
 
     def exchange(chips, first):
         @pl.loop(0, 4)
         def _(i2):
-            halves = []
-            for e in range(2):
-                halves.append(jnp.concatenate(
-                    [t4[pl.ds(pl.multiple_of(((2 * i2 + e) * OCC + k) * PITCH + chip * 24, 8), 24), :]
-                     for chip in chips for k in range(OCC)], axis=0))
-            rhs = jnp.concatenate(halves, axis=1).astype(BF16)
-            prod = jnp.dot(wxt[:, first * 384:(first + len(chips)) * 384], rhs, preferred_element_type=F32)
-            vbuf_s[i2, :, :] = prod if first == 0 else vbuf_s[i2, :, :] + prod
+            exchange_pair(chips, first, i2)
 
     direct(c)
 
     x0.wait_recv()
-    f0 = tcopy(nx, h0, 5, _dev(ny, r))
-    f0.start()
+    for p in range(4):
+        fcopy(nx, h0, 0, p, _dev(ny, r)).start()
     y1.wait_recv()
-    f1 = tcopy(ny, h1, 6, _dev(nx, r))
-    f1.start()
+    for p in range(4):
+        fcopy(ny, h1, 1, p, _dev(nx, r)).start()
     q = n // 4
     xcopies = []
     for s, cc in enumerate((nx, ny, dg)):
@@ -163,13 +177,29 @@
     direct(ny)
     exchange((c, nx, ny), 0)
 
-    f0.wait_recv()
-    f1.wait_recv()
+    @pl.loop(0, 4)
+    def _(p):
+        fcopy(dg, h0, 0, p, _dev(ny, r)).wait_recv()
+        fcopy(dg, h1, 1, p, _dev(nx, r)).wait_recv()
+        for ib in range(2):
+            spread_rows(dg, 2 * p + ib, 0, 6)
+        ubuf[dg, pl.ds(pl.multiple_of(p * 48, 16), 48), :] = direct_rows(dg, 2 * p, 2)
+        exchange_pair((dg,), 3, p)
+
     d_d = tcopy(dg, whole, 9, _dev(c, o))
     d_d.start()
-    spread(dg, 0, 6)
-    direct(dg)
-    exchange((dg,), 3)
+
+    for cp in xcopies:
+        cp.wait_recv()
+    xsum = (xr[0] + xr[1]) + (xr[2] + xr[3])
+    krows = pl.ds(pl.multiple_of(r * n + c * q, q), q)
+    mfull[krows, :] = (oooo[krows, :].astype(F32) + 0.5 * xsum).astype(BF16)
+    mcopies = []
+    for s, (cc, rr) in enumerate(((nx, r), (ny, r), (dg, r), (c, o), (nx, o), (ny, o), (dg, o))):
+        part_m = mfull.at[krows, pl.ds(pl.multiple_of(rr * n, n), n)]
+        cp = _rcopy(part_m, part_m, ms.at[s], mrs.at[s], _dev(cc, rr))
+        cp.start()
+        mcopies.append(cp)
 
     own = c // 2
     half = c % 2
@@ -215,18 +245,6 @@
             put(st4, c, pmsg.at[3, j])
             pcopy(j, 3).start()
 
-    for cp in xcopies:
-        cp.wait_recv()
-    xsum = (xr[0] + xr[1]) + (xr[2] + xr[3])
-    krows = pl.ds(pl.multiple_of(r * n + c * q, q), q)
-    mfull[krows, :] = (oooo[krows, :].astype(F32) + 0.5 * xsum).astype(BF16)
-    mcopies = []
-    for s, (cc, rr) in enumerate(((nx, r), (ny, r), (dg, r), (c, o), (nx, o), (ny, o), (dg, o))):
-        part_m = mfull.at[krows, pl.ds(pl.multiple_of(rr * n, n), n)]
-        cp = _rcopy(part_m, part_m, ms.at[s], mrs.at[s], _dev(cc, rr))
-        cp.start()
-        mcopies.append(cp)
-
     d_x.wait_recv()
     d_y.wait_recv()
     d_d.wait_recv()
@@ -253,8 +271,11 @@
     def _(s):
         ladder_copy(s).wait()
 
-    for cp in (d_own, x0, y1, x1, y0, f0, f1, d_x, d_y, d_d, *xcopies, *mcopies):
+    for cp in (d_own, x0, y1, x1, y0, d_x, d_y, d_d, *xcopies, *mcopies):
         cp.wait_send()
+    for p in range(4):
+        fcopy(nx, h0, 0, p, _dev(ny, r)).wait_send()
+        fcopy(ny, h1, 1, p, _dev(nx, r)).wait_send()
 
     for cp in mcopies:
         cp.wait_recv()
@@ -332,12 +353,12 @@
             V((8 * PITCH, LANE), F32), V((8 * PITCH, LANE), F32),
             V((3, 4, 8, w), F32), V((4, 4, 8, w), F32), V((4, 4, 8, w), F32), V((2, 2, 4, 8, w), F32),
             V((3, depth, STEP), BF16), V((n, w), F32), V((w // STEP, 2 * n, STEP), F32), V(wx.shape, F32),
-            DMA((5,)), DMA((10,)), DMA((10,)), DMA((3,)), DMA((3,)), DMA((7,)), DMA((7,)),
+            DMA((5,)), DMA((10,)), DMA((10,)), DMA((2, 4)), DMA((2, 4)), DMA((3,)), DMA((3,)), DMA((7,)), DMA((7,)),
             DMA((3, 4)), DMA((4, 4)), DMA((4, 4)), DMA((2, 2, 4)), DMA((3,)), DMA((w // STEP,)), DMA((w // STEP,)),
         ],
-        compiler_params=pltpu.CompilerParams(collective_id=0, has_side_effects=True, vmem_limit_bytes=60 << 20),
+        compiler_params=pltpu.CompilerParams(collective_id=0, has_side_effects=True, vmem_limit_bytes=46 << 20),
         name="sweep",
-    )(t, oovv, vvvv, oooo, wd, wx)
+    )(*(pltpu.with_memory_space_constraint(a, pltpu.HBM) for a in (t, oovv, vvvv, oooo, wd, wx)))
 
 
 def solution(mesh):

time: 63.1 us -> 57.2 us (0.906)
  Pallas kernels: 60.5 us -> 55.9 us
  other arithmetic: 2.44 us -> 1.17 us
    pallas_call x1, Pallas kernels: 60.5 us -> 55.9 us  [sweep(): pl.pallas_call(sweep_kernel, out_shape=jax.ShapeDtypeStruct((n, w), F32),...]
    div x1, other arithmetic: 2.44 us -> 1.17 us  [local_sweep(): return sweep(t_blk, oovv_blk, vvvv_blk, oooo_full, wd_blk, wx_blk) / d_blk]
where the time goes in v4:
time: 57.2 us; the launch traced here: 57.1 us
  Pallas kernels  55.9 us (98%)
  other arithmetic  1.17 us (2%)
    pallas_call x1, Pallas kernels, sweep(): pl.pallas_call(sweep_kernel, out_shape=jax.ShapeDtypeStruct((n, w), F32),...  55.9 us
    div x1, other arithmetic, local_sweep(): return sweep(t_blk, oovv_blk, vvvv_blk, oooo_full, wd_blk, wx_blk) / d_blk  1.17 us

profile of v4, /device:TPU:0, one launch (start us, length us, event | category | flops | bytes accessed | tf_op | source)
XLA Modules:
  0.0 57.1 jit_solution(10524256941184167056)
XLA Ops:
  0.0 0.0 copy-start
  0.0 55.9 %sweep.1 = f32[128,2304]{1,0:T(8,128)S(1)} custom-call(f32[128,2304]{1,0:T(8,128)} %t_hbm.1, bf16[128,2304]{1,0:T(8,128)(2,1)} %oovv_hbm.1, bf16[4608,2304]{1,0:T(8,128)(2,1)} %v_hbm.1, bf16[256,256]{1,0:T(8,128)(2,1)} %oooo_hbm.1, bf16[1536,384]{1,0:T(8,128)(2,1)} %wd_hbm.1, bf16[1536,384]{1,0:T(8,128)(2,1)} %wx_hbm.1), custom_call_target="tpu_custom_call" | custom-call | tf_op jit(solution)/shard_map/sweep/pallas_call | solution.py:342
  55.9 0.0 copy-done
  55.9 1.2 %div.3 = f32[128,2304]{1,0:T(8,128)} divide(f32[128,2304]{1,0:T(8,128)S(1)} %sweep.1, f32[128,2304]{1,0:T(8,128)S(1)} %copy-done) | non-fusion elementwise | flops 294912 | bytes 3538944 | tf_op jit(solution)/shard_map/div | solution.py:366
Async XLA Ops:
  0.0 55.9 %copy-start = (f32[128,2304]{1,0:T(8,128)S(1)}, f32[128,2304]{1,0:T(8,128)}, u32[]{:S(2)}) copy-start(f32[128,2304]{1,0:T(8,128)} %param.8) | copy-start | bytes 3538948

commit v5 on v4

--- a/solution.py
+++ b/solution.py
@@ -28,7 +28,7 @@
 
 def sweep_kernel(t_hbm, oovv_hbm, v_hbm, oooo_hbm, wd_hbm, wx_hbm, out_ref,
                  t32, oovv, oooo, wd, wx, tg, xp, xr, mfull, hole, t4, wd4, wxt, ubuf, vbuf_s, s4, st4,
-                 smsg, pmsg, srecv, precv, vv, theirs, part, wxf,
+                 smsg, pmsg, srecv, phome, pfar, vv, theirs, part, wxf,
                  lsem, gs, gr, fs, fr, xs, xrs, ms, mrs, ss, srs, ps, prs, vsem, rs, rrs):
     r, c = lax.axis_index("row"), lax.axis_index("col")
     x, y = c % 2, c // 2
@@ -189,6 +189,78 @@
     d_d = tcopy(dg, whole, 9, _dev(c, o))
     d_d.start()
 
+    own = c // 2
+    half = c % 2
+
+    def put(src, chip, dst, first=0, count=8):
+        for g in range(6):
+            vals = [src[pl.ds(first * PITCH + chip * 24 + g * 4 + e, count, stride=PITCH), :][:, :VIRT]
+                    for e in range(4)]
+            dst[:, g * 384:(g + 1) * 384] = jnp.concatenate(vals, axis=1)
+
+    dests = (dg, nx, ny)
+
+    def scopy(j, s):
+        return _rcopy(smsg.at[s, j], srecv.at[c, j], ss, srs, _dev(dests[s], r))
+
+    def hcopy(m, s):
+        return _rcopy(pmsg.at[s, m], phome.at[half, m], ps, prs.at[0, m], _dev(dests[s], r))
+
+    def pcopy(j, s):
+        chip = (dg, nx, ny, c)[s]
+        return _rcopy(pmsg.at[s, j], pfar.at[half, j], ps, prs.at[1, j], _dev(chip, o))
+
+    def block(i, j):
+        direct_part = jnp.concatenate(
+            [ubuf[chip, pl.ds(pl.multiple_of(i * 24, 8), 24), pl.ds(pl.multiple_of(j * LANE, LANE), LANE)]
+             for chip in range(4)], axis=0)
+        return direct_part - vbuf_s[
+            i // 2, pl.ds(pl.multiple_of(j * VIRT, 8), VIRT), pl.ds(pl.multiple_of((i % 2) * LANE, LANE), LANE)]
+
+    def send_s(j):
+        for i in range(8):
+            s4[i * PITCH:i * PITCH + VIRT, :] = block(i, j)
+
+        @pl.when(own == r)
+        def _():
+            for e in range(4):
+                at = pl.ds(pl.multiple_of((half * 4 + e) * PITCH, 8), VIRT)
+                s4[at, :VIRT] = s4[at, :VIRT] + block(half * 4 + j, e).T[:VIRT, :]
+
+        for s in range(3):
+            put(s4, dests[s], smsg.at[s, j])
+            scopy(j, s).start()
+        put(s4, c, srecv.at[c, j])
+
+    def send_p(j):
+        @pl.when(own != r)
+        def _():
+            for i in range(8):
+                st4[i * PITCH:i * PITCH + VIRT, :VIRT] = s4[i * PITCH:i * PITCH + VIRT, :].T[:VIRT, :]
+            for s in range(3):
+                put(st4, dests[s], pmsg.at[s, j])
+                pcopy(j, s).start()
+            put(st4, c, pmsg.at[3, j])
+            pcopy(j, 3).start()
+
+        @pl.when(own == r)
+        def _():
+            for e in range(4):
+                at = pl.ds(pl.multiple_of(((1 - half) * 4 + e) * PITCH, 8), VIRT)
+                to = pl.ds(pl.multiple_of(((j % 2) * 4 + e) * PITCH, 8), VIRT)
+                st4[to, :VIRT] = s4[at, :].T[:VIRT, :]
+
+            @pl.when(j % 2 == 1)
+            def _():
+                m = j // 2
+                for s in range(3):
+                    put(st4, dests[s], pmsg.at[s, m])
+                    hcopy(m, s).start()
+                put(st4, c, phome.at[half, m])
+
+    send_s(0)
+    send_p(0)
+
     for cp in xcopies:
         cp.wait_recv()
     xsum = (xr[0] + xr[1]) + (xr[2] + xr[3])
@@ -201,49 +273,10 @@
         cp.start()
         mcopies.append(cp)
 
-    own = c // 2
-    half = c % 2
-
-    def put(src, chip, dst):
-        for g in range(6):
-            vals = [src[pl.ds(chip * 24 + g * 4 + e, 8, stride=PITCH), :][:, :VIRT] for e in range(4)]
-            dst[:, g * 384:(g + 1) * 384] = jnp.concatenate(vals, axis=1)
-
-    dests = (dg, nx, ny)
-
-    def scopy(j, s):
-        return _rcopy(smsg.at[s, j], srecv.at[c, j], ss.at[s, j], srs.at[c, j], _dev(dests[s], r))
-
-    def pcopy(j, s):
-        chip = (dg, nx, ny, c)[s]
-        return _rcopy(pmsg.at[s, j], precv.at[half, r, j], ps.at[s, j], prs.at[half, r, j], _dev(chip, own))
-
-    @pl.loop(0, 4)
+    @pl.loop(1, 4)
     def _(j):
-        for i in range(8):
-            blk = jnp.concatenate(
-                [ubuf[chip, i * 24:(i + 1) * 24, pl.ds(pl.multiple_of(j * LANE, LANE), LANE)] for chip in range(4)],
-                axis=0)
-            s4[i * PITCH:i * PITCH + VIRT, :] = blk - vbuf_s[
-                i // 2, pl.ds(pl.multiple_of(j * VIRT, 8), VIRT), (i % 2) * LANE:(i % 2 + 1) * LANE]
-        for s in range(3):
-            put(s4, dests[s], smsg.at[s, j])
-            scopy(j, s).start()
-        for i in range(8):
-            st4[i * PITCH:i * PITCH + VIRT, :VIRT] = s4[i * PITCH:i * PITCH + VIRT, :].T[:VIRT, :]
-        for s in range(3):
-            put(st4, dests[s], pmsg.at[s, j])
-            pcopy(j, s).start()
-        put(s4, c, srecv.at[c, j])
-
-        @pl.when(own == r)
-        def _():
-            put(st4, c, precv.at[half, r, j])
-
-        @pl.when(own != r)
-        def _():
-            put(st4, c, pmsg.at[3, j])
-            pcopy(j, 3).start()
+        send_s(j)
+        send_p(j)
 
     d_x.wait_recv()
     d_y.wait_recv()
@@ -251,7 +284,7 @@
 
     def ladder_copy(s):
         lanes = pl.ds(pl.multiple_of(s * STEP, STEP), STEP)
-        return _rcopy(part.at[s, orows], theirs.at[:, lanes], rs.at[s], rrs.at[s], _dev(c, o))
+        return _rcopy(part.at[s, orows], theirs.at[:, lanes], rs, rrs, _dev(c, o))
 
     @pl.loop(0, w // STEP)
     def _(s):
@@ -267,9 +300,11 @@
                          + jnp.dot(tg[2 * r + 1], vb[...], preferred_element_type=F32))
         ladder_copy(s).start()
 
-    @pl.loop(0, w // STEP)
-    def _(s):
-        ladder_copy(s).wait()
+    def landed(like, sem):
+        return pltpu.make_async_copy(like, like, sem)
+
+    landed(theirs, rrs).wait()
+    landed(theirs, rs).wait()
 
     for cp in (d_own, x0, y1, x1, y0, d_x, d_y, d_d, *xcopies, *mcopies):
         cp.wait_send()
@@ -293,42 +328,47 @@
         mine = jnp.concatenate([part[s, line_r, :] for s in range(w // STEP)], axis=1)
         out_ref[line, :] = oovv[line, :].astype(F32) + (mine + theirs[line, :] + hole[line, :])
 
-    for s in range(3):
-        @pl.loop(0, 4)
-        def _(j):
-            scopy(j, s).wait_send()
-            pcopy(j, s).wait_send()
-
-    @pl.when(own != r)
-    def _():
-        @pl.loop(0, 4)
-        def _(j):
-            pcopy(j, 3).wait_send()
-
-    def landed(dst, sem):
-        return pltpu.make_async_copy(dst, dst, sem)
-
-    for a, chip in enumerate((nx, ny, dg)):
-        @pl.loop(0, 4)
-        def _(j):
-            landed(srecv.at[chip, j], srs.at[chip, j]).wait()
-
-    for a in range(2):
-        for b in range(2):
-            here = jnp.logical_and(c == 2 * r + a, r == b)
-
-            @pl.when(jnp.logical_not(here))
-            def _():
-                @pl.loop(0, 4)
-                def _(j):
-                    landed(precv.at[a, b, j], prs.at[a, b, j]).wait()
-
+    landed(srecv.at[pl.ds(0, 3)], srs).wait()
+    landed(smsg, ss).wait()
     @pl.loop(0, 8)
     def _(i):
         for jh in range(2):
             line = pl.ds(pl.multiple_of(i * 16 + jh * 8, 8), 8)
             sv = jnp.concatenate([srecv.at[2 * jh + e // 4, e % 4][pl.ds(i, 1), :] for e in range(8)], axis=0)
-            out_ref[line, :] = out_ref[line, :] + (sv + precv[i // 4, jh, i % 4])
+            out_ref[line, :] = out_ref[line, :] + sv
+
+    mate = own == r
+    zero4 = jnp.zeros((4, w), F32)
+    for j in range(4):
+        landed(pfar.at[:, j], prs.at[1, j]).wait()
+        for a in range(2):
+            line = pl.ds(pl.multiple_of((a * 4 + j) * 16 + o * 8, 8), 8)
+            out_ref[line, :] = out_ref[line, :] + pfar[a, j]
+        if j % 2 == 1:
+            m = j // 2
+
+            @pl.when(mate)
+            def _():
+                landed(phome.at[0, m], prs.at[0, m]).wait()
+
+            @pl.when(jnp.logical_not(mate))
+            def _():
+                landed(phome.at[:, m], prs.at[0, m]).wait()
+
+            for jj in (j - 1, j):
+                for a in range(2):
+                    line = pl.ds(pl.multiple_of((a * 4 + jj) * 16 + r * 8, 8), 8)
+                    rest = phome[a, m, (jj % 2) * 4:(jj % 2) * 4 + 4, :]
+                    both = (zero4, rest) if a == 0 else (rest, zero4)
+                    out_ref[line, :] = out_ref[line, :] + jnp.concatenate(both, axis=0)
+
+    @pl.when(mate)
+    def _():
+        landed(pmsg.at[pl.ds(0, 3), pl.ds(0, 2)], ps).wait()
+
+    @pl.when(jnp.logical_not(mate))
+    def _():
+        landed(pmsg, ps).wait()
 
 
 ANY = pl.BlockSpec(memory_space=pl.ANY)
@@ -351,10 +391,10 @@
             V((n * PITCH, LANE), F32), V((OCC * LANE, 4 * LANE), BF16), V((wx.shape[1], wx.shape[0]), BF16),
             V((4, 2 * VIRT, 4 * LANE), F32), V((4, 4 * VIRT, 2 * LANE), F32),
             V((8 * PITCH, LANE), F32), V((8 * PITCH, LANE), F32),
-            V((3, 4, 8, w), F32), V((4, 4, 8, w), F32), V((4, 4, 8, w), F32), V((2, 2, 4, 8, w), F32),
+            V((3, 4, 8, w), F32), V((4, 4, 8, w), F32), V((4, 4, 8, w), F32), V((2, 2, 8, w), F32), V((2, 4, 8, w), F32),
             V((3, depth, STEP), BF16), V((n, w), F32), V((w // STEP, 2 * n, STEP), F32), V(wx.shape, F32),
             DMA((5,)), DMA((10,)), DMA((10,)), DMA((2, 4)), DMA((2, 4)), DMA((3,)), DMA((3,)), DMA((7,)), DMA((7,)),
-            DMA((3, 4)), DMA((4, 4)), DMA((4, 4)), DMA((2, 2, 4)), DMA((3,)), DMA((w // STEP,)), DMA((w // STEP,)),
+            DMA, DMA, DMA, DMA((2, 4)), DMA((3,)), DMA, DMA,
         ],
         compiler_params=pltpu.CompilerParams(collective_id=0, has_side_effects=True, vmem_limit_bytes=46 << 20),
         name="sweep",

time: 57.2 us -> 52.4 us (0.916)
  Pallas kernels: 55.9 us -> 51.1 us
    pallas_call x1, Pallas kernels: 55.9 us -> 51.1 us  [sweep(): pl.pallas_call(sweep_kernel, out_shape=jax.ShapeDtypeStruct((n, w), F32),...]
where the time goes in v5:
time: 52.4 us; the launch traced here: 52.2 us
  Pallas kernels  51.1 us (98%)
  other arithmetic  1.17 us (2%)
    pallas_call x1, Pallas kernels, sweep(): pl.pallas_call(sweep_kernel, out_shape=jax.ShapeDtypeStruct((n, w), F32),...  51.1 us
    div x1, other arithmetic, local_sweep(): return sweep(t_blk, oovv_blk, vvvv_blk, oooo_full, wd_blk, wx_blk) / d_blk  1.17 us

profile of v5, /device:TPU:0, one launch (start us, length us, event | category | flops | bytes accessed | tf_op | source)
XLA Modules:
  0.0 52.2 jit_solution(6367077603382444372)
XLA Ops:
  0.0 0.0 copy-start
  0.0 51.1 %sweep.1 = f32[128,2304]{1,0:T(8,128)S(1)} custom-call(f32[128,2304]{1,0:T(8,128)} %t_hbm.1, bf16[128,2304]{1,0:T(8,128)(2,1)} %oovv_hbm.1, bf16[4608,2304]{1,0:T(8,128)(2,1)} %v_hbm.1, bf16[256,256]{1,0:T(8,128)(2,1)} %oooo_hbm.1, bf16[1536,384]{1,0:T(8,128)(2,1)} %wd_hbm.1, bf16[1536,384]{1,0:T(8,128)(2,1)} %wx_hbm.1), custom_call_target="tpu_custom_call" | custom-call | tf_op jit(solution)/shard_map/sweep/pallas_call | solution.py:382
  51.1 0.0 copy-done
  51.1 1.2 %div.3 = f32[128,2304]{1,0:T(8,128)} divide(f32[128,2304]{1,0:T(8,128)S(1)} %sweep.1, f32[128,2304]{1,0:T(8,128)S(1)} %copy-done) | non-fusion elementwise | flops 294912 | bytes 3538944 | tf_op jit(solution)/shard_map/div | solution.py:406
Async XLA Ops:
  0.0 51.1 %copy-start = (f32[128,2304]{1,0:T(8,128)S(1)}, f32[128,2304]{1,0:T(8,128)}, u32[]{:S(2)}) copy-start(f32[128,2304]{1,0:T(8,128)} %param.8) | copy-start | bytes 3538948

commit v6 on v4

v6 whole, which is shorter than its diff:
```python
import jax
import jax.numpy as jnp
from jax import lax
from jax.experimental import pallas as pl
from jax.experimental.pallas import tpu as pltpu
from jax.sharding import PartitionSpec as P

MESH = pl.DeviceIdType.MESH
F32 = jnp.float32
BF16 = jnp.bfloat16
NT = (((1,), (1,)), ((), ()))
TN = (((0,), (0,)), ((), ()))

OCC = 16
VIRT = 96
LANE = 128
PITCH = 104
STEP = 256


def _dev(c, r):
    return {"col": c, "row": r}


def _rcopy(src, dst, ssem, rsem, dev):
    return pltpu.make_async_remote_copy(src, dst, ssem, rsem, device_id=dev, device_id_type=MESH)


def sweep_kernel(t_hbm, oovv_hbm, v_hbm, oooo_hbm, wd_hbm, wx_hbm, out_ref,
                 t32, oovv, oooo, ww, tg, xp, xr, mfull, hole, t4, wd4, wxt, ubuf, vbuf_s, s4, st4,
                 smsg, pmsg, srecv, precv, rmsg, rrecv, vv, theirs, part, wxf,
                 lsem, gs, gr, fs, fr, xs, xrs, ms, mrs, ss, srs, ps, prs, rls, rlr, vsem, rs, rrs):
    r, c = lax.axis_index("row"), lax.axis_index("col")
    x, y = c % 2, c // 2
    o = 1 - r
    nx, ny, dg = y * 2 + (1 - x), (1 - y) * 2 + x, (1 - y) * 2 + (1 - x)
    n, w = t32.shape
    h = w // 2
    h0, h1 = pl.ds(0, h), pl.ds(h, h)
    rows = pl.ds(pl.multiple_of(r * n, n), n)
    orows = pl.ds(pl.multiple_of(o * n, n), n)

    chunk = n // 4
    tloads = [pltpu.make_async_copy(t_hbm.at[pl.ds(k * chunk, chunk)], t32.at[pl.ds(k * chunk, chunk)], lsem.at[k])
              for k in range(4)]
    for cp in tloads:
        cp.start()
    oload = pltpu.make_async_copy(oovv_hbm, oovv, lsem.at[4])
    hload = pltpu.make_async_copy(oooo_hbm, oooo, lsem.at[5])
    wloads = [pltpu.make_async_copy(a, ww.at[k], lsem.at[6]) for k, a in enumerate((wd_hbm, wx_hbm))]
    for cp in (*wloads, oload, hload):
        cp.start()

    own = c // 2
    half = c % 2
    home = (own + r + 1) % 2
    via = home * nx + (1 - home) * ny
    past = home * ny + (1 - home) * nx
    ro = (home + half) % 2
    di = 1 - ro

    def slot_s(chip, ih, m):
        return pl.ds(pl.multiple_of(((chip * 2 + ih) * 2 + m) * 8, 8), 8)

    def slot_p(kind, a, ih, m):
        return ((kind * 2 + a) * 2 + ih) * 2 + m

    zero8 = jnp.zeros((8, w), F32)
    for m in range(2):
        srecv[slot_s(dg, ro, m), :] = zero8
        precv[slot_p(0, 1 - half, half, m)] = zero8
        precv[slot_p(1, 1 - half, 1 - half, m)] = zero8

    sem = pltpu.get_barrier_semaphore()
    for cc, rr in ((nx, r), (ny, r), (dg, r), (c, o), (nx, o), (ny, o), (dg, o)):
        pl.semaphore_signal(sem, inc=1, device_id=_dev(cc, rr), device_id_type=MESH)

    def vcopy(s, slot):
        lanes = pl.ds(pl.multiple_of(s * STEP, STEP), STEP)
        return pltpu.make_async_copy(v_hbm.at[:, lanes], vv.at[slot], vsem.at[slot])

    def landed(like, sem):
        return pltpu.make_async_copy(like, like, sem)

    for k in range(4):
        tloads[k].wait()
        tg[c, pl.ds(pl.multiple_of(r * n + k * chunk, chunk), chunk), :] = t32[k * chunk:(k + 1) * chunk, :].astype(BF16)

    pl.semaphore_wait(sem, 7)

    def tcopy(chip, lanes, k, dev):
        ref = tg.at[chip, rows, lanes]
        return _rcopy(ref, ref, gs, gr.at[k], dev)

    def fcopy(chip, lanes, p, dev):
        ref = tg.at[chip, pl.ds(pl.multiple_of(r * n + p * 32, 32), 32), lanes]
        return _rcopy(ref, ref, fs, fr.at[p], dev)

    whole = pl.ds(0, w)
    x0 = tcopy(c, h0, 1, _dev(nx, r))
    y1 = tcopy(c, h1, 2, _dev(ny, r))
    d_own = tcopy(c, whole, 0, _dev(c, o))
    x1 = tcopy(c, h1, 3, _dev(nx, r))
    y0 = tcopy(c, h0, 4, _dev(ny, r))
    x0.start()
    y1.start()
    d_own.start()
    x1.start()
    y0.start()
    vcopy(0, 0).start()
    vcopy(1, 1).start()

    def spread_rows(chip, ib, first, groups):
        for g in range(first, first + groups):
            tile = tg[chip, pl.ds(pl.multiple_of(r * n + ib * 16, 16), 16), g * 384:(g + 1) * 384].astype(F32)
            for e in range(4):
                slab = tile[:, e * VIRT:(e + 1) * VIRT]
                slab = jnp.concatenate([slab, jnp.zeros((16, LANE - VIRT), F32)], axis=1)
                for half in range(2):
                    start = (ib * 16 + half * 8) * PITCH + chip * 24 + g * 4 + e
                    t4[pl.ds(start, 8, stride=PITCH), :] = slab[half * 8:half * 8 + 8]

    def spread(chip, first, groups):
        @pl.loop(0, n // 16)
        def _(ib):
            spread_rows(chip, ib, first, groups)

    spread(c, 0, 6)

    landed(ww, lsem.at[6]).wait()
    zrow = jnp.zeros((LANE - VIRT, 4 * LANE), BF16)

    @pl.loop(0, OCC)
    def _(k):
        blk = ww[0, pl.ds(pl.multiple_of(k * VIRT, 16), VIRT), :].astype(F32)
        parts = []
        for j in range(4):
            parts += [blk[:, j * VIRT:(j + 1) * VIRT], jnp.zeros((VIRT, LANE - VIRT), F32)]
        wd4[pl.ds(pl.multiple_of(k * LANE, LANE), VIRT), :] = jnp.concatenate(parts, axis=1).astype(BF16)
        wd4[pl.ds(pl.multiple_of(k * LANE + VIRT, 32), LANE - VIRT), :] = zrow
        wxf[pl.ds(pl.multiple_of(k * VIRT, 16), VIRT), :] = ww[1, pl.ds(pl.multiple_of(k * VIRT, 16), VIRT), :].astype(F32)

    for s, chip in enumerate((c, nx, ny, dg)):
        for b in range(3):
            blk = jnp.concatenate(
                [wxf[pl.ds(pl.multiple_of(k * VIRT + chip * 24, 8), 24), b * LANE:(b + 1) * LANE] for k in range(OCC)],
                axis=0)
            wxt[b * LANE:(b + 1) * LANE, s * 384:(s + 1) * 384] = blk.astype(BF16).T

    oload.wait()
    hload.wait()
    d_own.wait_recv()
    xp[...] = lax.dot_general(oovv[...], tg[c], NT, preferred_element_type=F32)

    def direct_rows(chip, i0, count):
        lhs = jnp.concatenate(
            [jnp.concatenate(
                [t4[pl.ds(pl.multiple_of(((i0 + i) * OCC + k) * PITCH + chip * 24, 8), 24), :] for i in range(count)],
                axis=0)
             for k in range(OCC)], axis=1).astype(BF16)
        return jnp.dot(lhs, wd4[...], preferred_element_type=F32)

    def direct(chip):
        ubuf[chip, :, :] = direct_rows(chip, 0, 8)

    def exchange_pair(chips, first, i2):
        halves = []
        for e in range(2):
            halves.append(jnp.concatenate(
                [t4[pl.ds(pl.multiple_of(((2 * i2 + e) * OCC + k) * PITCH + chip * 24, 8), 24), :]
                 for chip in chips for k in range(OCC)], axis=0))
        rhs = jnp.concatenate(halves, axis=1).astype(BF16)
        prod = jnp.dot(wxt[:, first * 384:(first + len(chips)) * 384], rhs, preferred_element_type=F32)
        vbuf_s[i2, :, :] = prod if first == 0 else vbuf_s[i2, :, :] + prod

    def exchange(chips, first):
        @pl.loop(0, 4)
        def _(i2):
            exchange_pair(chips, first, i2)

    direct(c)

    x0.wait_recv()
    for p in range(4):
        fcopy(nx, h0, p, _dev(ny, r)).start()
    y1.wait_recv()
    for p in range(4):
        fcopy(ny, h1, p, _dev(nx, r)).start()
    q = n // 4
    for cc in (nx, ny, dg):
        cp = _rcopy(xp.at[pl.ds(pl.multiple_of(cc * q, q), q)], xr.at[c], xs, xrs, _dev(cc, r))
        cp.start()
    xr[c, :, :] = xp[pl.ds(pl.multiple_of(c * q, q), q), :]
    spread(nx, 0, 3)
    spread(ny, 3, 3)
    x1.wait_recv()
    d_x = tcopy(nx, whole, 5, _dev(c, o))
    d_x.start()
    y0.wait_recv()
    d_y = tcopy(ny, whole, 5, _dev(c, o))
    d_y.start()
    spread(nx, 3, 3)
    spread(ny, 0, 3)
    direct(nx)
    direct(ny)
    exchange((c, nx, ny), 0)

    @pl.loop(0, 4)
    def _(p):
        landed(tg.at[dg, pl.ds(0, n // 4)], fr.at[p]).wait()
        for ib in range(2):
            spread_rows(dg, 2 * p + ib, 0, 6)
        ubuf[dg, pl.ds(pl.multiple_of(p * 48, 16), 48), :] = direct_rows(dg, 2 * p, 2)
        exchange_pair((dg,), 3, p)

    d_d = tcopy(dg, whole, 5, _dev(c, o))
    d_d.start()

    def row_of(ih, j, e):
        return pl.multiple_of((((j // 2) * 2 + ih) * 8 + (j % 2) * 4 + e) * PITCH, 8)

    def block(i, j):
        direct_part = jnp.concatenate(
            [ubuf[chip, pl.ds(pl.multiple_of(i * 24, 8), 24), pl.ds(pl.multiple_of(j * LANE, LANE), LANE)]
             for chip in range(4)], axis=0)
        return direct_part - vbuf_s[
            i // 2, pl.ds(pl.multiple_of(j * VIRT, 8), VIRT), pl.ds(pl.multiple_of((i % 2) * LANE, LANE), LANE)]

    def fill_s(ih):
        @pl.loop(0, 4)
        def _(j):
            for e in range(4):
                s4[pl.ds(row_of(ih, j, e), VIRT), :] = block(ih * 4 + e, j)

    def fill_t(ih):
        @pl.loop(0, 4)
        def _(j):
            for e in range(4):
                at = pl.ds(row_of(ih, j, e), VIRT)
                st4[at, :VIRT] = s4[at, :].T[:VIRT, :]

    def put(src, ih, m, chip, dst):
        first = ((m * 2 + ih) * 8) * PITCH + chip * 24
        for g in range(6):
            vals = [src[pl.ds(first + g * 4 + e, 8, stride=PITCH), :][:, :VIRT] for e in range(4)]
            dst[:, g * 384:(g + 1) * 384] = jnp.concatenate(vals, axis=1)

    def s_copy(slot, ih, m, chip):
        buf = smsg.at[slot * 4 + ih * 2 + m]
        return _rcopy(buf, srecv.at[slot_s(c, ih, m)], ss, srs, _dev(chip, r))

    def p_copy(slot, ih, m, chip):
        buf = pmsg.at[slot * 4 + ih * 2 + m]
        return _rcopy(buf, precv.at[slot_p(1 - home, half, ih, m)], ps, prs, _dev(chip, own))

    def relay(kind, src):
        @pl.loop(0, 2)
        def _(m):
            put(src, ro, m, dg, rmsg.at[kind * 2 + m])
            to = rrecv.at[pl.ds(pl.multiple_of((kind * 2 + m) * 8, 8), 8)]
            _rcopy(rmsg.at[kind * 2 + m], to, rls, rlr, _dev(via, own)).start()

    def send(src, msg, copy, slot, ih, chip):
        @pl.loop(0, 2)
        def _(m):
            put(src, ih, m, chip, msg.at[slot * 4 + ih * 2 + m])
            copy(slot, ih, m, chip).start()

    fill_s(ro)
    relay(0, s4)
    fill_t(ro)
    relay(1, st4)
    send(s4, smsg, s_copy, 1, ro, via)
    send(st4, pmsg, p_copy, 1, ro, via)

    landed(xr.at[pl.ds(0, 3)], xrs).wait()
    xsum = (xr[0] + xr[1]) + (xr[2] + xr[3])
    krows = pl.ds(pl.multiple_of(r * n + c * q, q), q)
    mfull[krows, :] = (oooo[krows, :].astype(F32) + 0.5 * xsum).astype(BF16)
    for cc, rr in ((nx, r), (ny, r), (dg, r), (c, o), (nx, o), (ny, o), (dg, o)):
        part_m = mfull.at[krows, pl.ds(pl.multiple_of(rr * n, n), n)]
        _rcopy(part_m, part_m, ms, mrs, _dev(cc, rr)).start()

    fill_s(di)

    @pl.when(home == 1)
    def _():
        @pl.loop(0, 4)
        def _(j):
            for e in range(4):
                at = pl.ds(row_of(di, j, e), VIRT)
                s4[at, :VIRT] = s4[at, :VIRT] + block(half * 4 + j, e).T[:VIRT, :]

    send(s4, smsg, s_copy, 0, di, dg)
    send(s4, smsg, s_copy, 1, di, via)
    send(s4, smsg, s_copy, 2, di, past)

    @pl.when(home == 0)
    def _():
        fill_t(di)
        send(st4, pmsg, p_copy, 0, di, dg)
        send(st4, pmsg, p_copy, 1, di, via)
        send(st4, pmsg, p_copy, 2, di, past)
        send(st4, pmsg, p_copy, 3, ro, c)
        send(st4, pmsg, p_copy, 3, di, c)

    @pl.loop(0, 2)
    def _(m):
        for ih in range(2):
            put(s4, ih, m, c, srecv.at[slot_s(c, ih, m)])

    @pl.when(home == 1)
    def _():
        @pl.loop(0, 2)
        def _(m):
            put(st4, ro, m, c, precv.at[slot_p(0, half, ro, m)])

    def every_fourth(ref, first):
        return jnp.concatenate([ref[pl.ds(first + 4 * k, 1), :] for k in range(4)], axis=0)

    def pass_on():
        landed(rrecv, rlr).wait()
        for kind, (src, msg, copy) in ((1, (s4, smsg, s_copy)), (0, (st4, pmsg, p_copy))):
            for m in range(2):
                buf = msg.at[2 * 4 + ro * 2 + m]
                put(src, ro, m, past, buf)
                extra = jnp.concatenate([every_fourth(rrecv, kind * 16 + 2 * m + k) for k in range(2)], axis=0)
                buf[...] = buf[...] + extra
                copy(2, ro, m, past).start()

    landed(tg.at[pl.ds(0, 3), pl.ds(0, n)], gr.at[5]).wait()

    def ladder_copy(s):
        lanes = pl.ds(pl.multiple_of(s * STEP, STEP), STEP)
        return _rcopy(part.at[s, orows], theirs.at[:, lanes], rs, rrs, _dev(c, o))

    @pl.loop(0, w // STEP)
    def _(s):
        slot = s % 3

        @pl.when(s + 2 < w // STEP)
        def _():
            vcopy(s + 2, (s + 2) % 3).start()

        vcopy(s, slot).wait()
        va, vb = vv.at[slot, pl.ds(0, w)], vv.at[slot, pl.ds(w, w)]
        part[s, :, :] = (jnp.dot(tg[2 * r], va[...], preferred_element_type=F32)
                         + jnp.dot(tg[2 * r + 1], vb[...], preferred_element_type=F32))
        ladder_copy(s).start()

        @pl.when(s == 5)
        def _():
            pass_on()

    landed(theirs, rrs).wait()
    landed(theirs, rs).wait()

    landed(tg.at[pl.ds(0, 3)], gs).wait()
    landed(tg.at[0, pl.ds(0, n)], fs).wait()
    landed(xr.at[pl.ds(0, 3)], xs).wait()
    all_m = mfull.at[pl.ds(0, 7 * q), pl.ds(0, n)]
    landed(all_m, mrs).wait()
    landed(all_m, ms).wait()
    m_mine = mfull[:, rows]

    @pl.loop(0, w // STEP)
    def _(s):
        lanes = pl.ds(pl.multiple_of(s * STEP, STEP), STEP)
        hole[:, lanes] = lax.dot_general(m_mine, tg[c, :, lanes], TN, preferred_element_type=F32)

    @pl.loop(0, 8)
    def _(i):
        line = pl.ds(pl.multiple_of(i * 16, 16), 16)
        line_r = pl.ds(pl.multiple_of(r * n + i * 16, 16), 16)
        mine = jnp.concatenate([part[s, line_r, :] for s in range(w // STEP)], axis=1)
        out_ref[line, :] = oovv[line, :].astype(F32) + (mine + theirs[line, :] + hole[line, :])

    landed(rmsg, rls).wait()
    landed(srecv.at[pl.ds(0, 80)], srs).wait()
    @pl.loop(0, 8)
    def _(i):
        for jh in range(2):
            line = pl.ds(pl.multiple_of(i * 16 + jh * 8, 8), 8)
            sv = jnp.concatenate(
                [every_fourth(srecv, ((2 * jh + cc) * 2 + i // 4) * 16 + i % 4) for cc in range(2)], axis=0)
            out_ref[line, :] = out_ref[line, :] + sv

    @pl.when(home == 1)
    def _():
        landed(precv.at[pl.ds(0, 10)], prs).wait()

    @pl.when(home == 0)
    def _():
        landed(precv.at[pl.ds(0, 8)], prs).wait()

    zero4 = jnp.zeros((4, w), F32)
    for a in range(2):
        for j in range(4):
            m, rows4 = j // 2, slice(j % 2 * 4, j % 2 * 4 + 4)
            for kind, row in ((0, r), (1, o)):
                line = pl.ds(pl.multiple_of((a * 4 + j) * 16 + row * 8, 8), 8)
                both = [zero4 if kind == 0 and ih == a else precv[slot_p(kind, a, ih, m), rows4, :] for ih in range(2)]
                out_ref[line, :] = out_ref[line, :] + jnp.concatenate(both, axis=0)

    landed(smsg.at[pl.ds(0, 10)], ss).wait()

    @pl.when(home == 1)
    def _():
        landed(pmsg.at[pl.ds(0, 4)], ps).wait()

    @pl.when(home == 0)
    def _():
        landed(pmsg.at[pl.ds(0, 14)], ps).wait()


ANY = pl.BlockSpec(memory_space=pl.ANY)
DMA = pltpu.SemaphoreType.DMA


def sweep(t, oovv, vvvv, oooo, wd, wx):
    n, w = t.shape
    depth = vvvv.shape[0]
    V = pltpu.VMEM
    return pl.pallas_call(
        sweep_kernel,
        out_shape=jax.ShapeDtypeStruct((n, w), F32),
        in_specs=[ANY] * 6,
        out_specs=pl.BlockSpec(memory_space=pltpu.VMEM),
        scratch_shapes=[
            V((n, w), F32), V((n, w), BF16), V(oooo.shape, BF16), V((2,) + wd.shape, BF16),
            V((4, 2 * n, w), BF16),
            V((n, 2 * n), F32), V((4, n // 4, 2 * n), F32), V((2 * n, 2 * n), BF16), V((n, w), F32),
            V((n * PITCH, LANE), F32), V((OCC * LANE, 4 * LANE), BF16), V((wx.shape[1], wx.shape[0]), BF16),
            V((4, 2 * VIRT, 4 * LANE), F32), V((4, 4 * VIRT, 2 * LANE), F32),
            V((32 * PITCH, LANE), F32), V((32 * PITCH, LANE), F32),
            V((12, 8, w), F32), V((16, 8, w), F32), V((128, w), F32), V((16, 8, w), F32), V((4, 8, w), F32), V((32, w), F32),
            V((3, depth, STEP), BF16), V((n, w), F32), V((w // STEP, 2 * n, STEP), F32), V(wx.shape, F32),
            DMA((7,)), DMA, DMA((6,)), DMA, DMA((4,)), DMA, DMA, DMA, DMA,
            DMA, DMA, DMA, DMA, DMA, DMA, DMA((3,)), DMA, DMA,
        ],
        compiler_params=pltpu.CompilerParams(collective_id=0, has_side_effects=True, vmem_limit_bytes=46 << 20),
        name="sweep",
    )(*(pltpu.with_memory_space_constraint(a, pltpu.HBM) for a in (t, oovv, vvvv, oooo, wd, wx)))


def solution(mesh):
    def local_sweep(t_blk, d_blk, oovv_blk, vvvv_blk, oooo_full, wd_blk, wx_blk):
        return sweep(t_blk, oovv_blk, vvvv_blk, oooo_full, wd_blk, wx_blk) / d_blk

    amp = P("row", "col")
    wide = P(None, "col")
    return jax.shard_map(local_sweep, mesh=mesh, in_specs=(amp, amp, amp, amp, P(), wide, wide), out_specs=amp, check_vma=False)
```

time: 57.2 us -> 51.2 us (0.90)
  Pallas kernels: 55.9 us -> 49.9 us
    pallas_call x1, Pallas kernels: 55.9 us -> 49.9 us  [sweep(): pl.pallas_call(sweep_kernel, out_shape=jax.ShapeDtypeStruct((n, w), F32),...]
where the time goes in v6:
time: 51.2 us; the launch traced here: 51.1 us
  Pallas kernels  49.9 us (97%)
  other arithmetic  1.17 us (2%)
    pallas_call x1, Pallas kernels, sweep(): pl.pallas_call(sweep_kernel, out_shape=jax.ShapeDtypeStruct((n, w), F32),...  49.9 us
    div x1, other arithmetic, local_sweep(): return sweep(t_blk, oovv_blk, vvvv_blk, oooo_full, wd_blk, wx_blk) / d_blk  1.17 us

profile of v6, /device:TPU:0, one launch (start us, length us, event | category | flops | bytes accessed | tf_op | source)
XLA Modules:
  0.0 51.1 jit_solution(14169031020746917470)
XLA Ops:
  0.0 0.0 copy-start
  0.0 49.9 %sweep.1 = f32[128,2304]{1,0:T(8,128)S(1)} custom-call(f32[128,2304]{1,0:T(8,128)} %t_hbm.1, bf16[128,2304]{1,0:T(8,128)(2,1)} %oovv_hbm.1, bf16[4608,2304]{1,0:T(8,128)(2,1)} %v_hbm.1, bf16[256,256]{1,0:T(8,128)(2,1)} %oooo_hbm.1, bf16[1536,384]{1,0:T(8,128)(2,1)} %wd_hbm.1, bf16[1536,384]{1,0:T(8,128)(2,1)} %wx_hbm.1), custom_call_target="tpu_custom_call" | custom-call | tf_op jit(solution)/shard_map/sweep/pallas_call | solution.py:424
  49.9 0.0 copy-done
  49.9 1.2 %div.3 = f32[128,2304]{1,0:T(8,128)} divide(f32[128,2304]{1,0:T(8,128)S(1)} %sweep.1, f32[128,2304]{1,0:T(8,128)S(1)} %copy-done) | non-fusion elementwise | flops 294912 | bytes 3538944 | tf_op jit(solution)/shard_map/div | solution.py:448
Async XLA Ops:
  0.0 49.9 %copy-start = (f32[128,2304]{1,0:T(8,128)S(1)}, f32[128,2304]{1,0:T(8,128)}, u32[]{:S(2)}) copy-start(f32[128,2304]{1,0:T(8,128)} %param.8) | copy-start | bytes 3538948

commit v7 on v6

--- a/solution.py
+++ b/solution.py
@@ -216,8 +216,11 @@
     d_d = tcopy(dg, whole, 5, _dev(c, o))
     d_d.start()
 
-    def row_of(ih, j, e):
-        return pl.multiple_of((((j // 2) * 2 + ih) * 8 + (j % 2) * 4 + e) * PITCH, 8)
+    def s_rows(i, j):
+        return pl.ds(pl.multiple_of((i * 4 + j) * PITCH, 8), VIRT)
+
+    def t_rows(i, j):
+        return pl.ds(pl.multiple_of(((i // 4) * 16 + j * 4 + i % 4) * PITCH, 8), VIRT)
 
     def block(i, j):
         direct_part = jnp.concatenate(
@@ -230,17 +233,16 @@
         @pl.loop(0, 4)
         def _(j):
             for e in range(4):
-                s4[pl.ds(row_of(ih, j, e), VIRT), :] = block(ih * 4 + e, j)
+                s4[s_rows(ih * 4 + e, j), :] = block(ih * 4 + e, j)
 
     def fill_t(ih):
         @pl.loop(0, 4)
         def _(j):
             for e in range(4):
-                at = pl.ds(row_of(ih, j, e), VIRT)
-                st4[at, :VIRT] = s4[at, :].T[:VIRT, :]
+                st4[t_rows(ih * 4 + e, j), :VIRT] = s4[s_rows(ih * 4 + e, j), :].T[:VIRT, :]
 
     def put(src, ih, m, chip, dst):
-        first = ((m * 2 + ih) * 8) * PITCH + chip * 24
+        first = (ih * 16 + m * 8) * PITCH + chip * 24
         for g in range(6):
             vals = [src[pl.ds(first + g * 4 + e, 8, stride=PITCH), :][:, :VIRT] for e in range(4)]
             dst[:, g * 384:(g + 1) * 384] = jnp.concatenate(vals, axis=1)
@@ -270,8 +272,6 @@
     relay(0, s4)
     fill_t(ro)
     relay(1, st4)
-    send(s4, smsg, s_copy, 1, ro, via)
-    send(st4, pmsg, p_copy, 1, ro, via)
 
     landed(xr.at[pl.ds(0, 3)], xrs).wait()
     xsum = (xr[0] + xr[1]) + (xr[2] + xr[3])
@@ -288,19 +288,17 @@
         @pl.loop(0, 4)
         def _(j):
             for e in range(4):
-                at = pl.ds(row_of(di, j, e), VIRT)
+                at = s_rows(half * 4 + e, j)
                 s4[at, :VIRT] = s4[at, :VIRT] + block(half * 4 + j, e).T[:VIRT, :]
 
+    send(s4, smsg, s_copy, 2, di, past)
     send(s4, smsg, s_copy, 0, di, dg)
-    send(s4, smsg, s_copy, 1, di, via)
-    send(s4, smsg, s_copy, 2, di, past)
 
     @pl.when(home == 0)
     def _():
         fill_t(di)
+        send(st4, pmsg, p_copy, 2, di, past)
         send(st4, pmsg, p_copy, 0, di, dg)
-        send(st4, pmsg, p_copy, 1, di, via)
-        send(st4, pmsg, p_copy, 2, di, past)
         send(st4, pmsg, p_copy, 3, ro, c)
         send(st4, pmsg, p_copy, 3, di, c)
 
@@ -314,9 +312,6 @@
         @pl.loop(0, 2)
         def _(m):
             put(st4, ro, m, c, precv.at[slot_p(0, half, ro, m)])
-
-    def every_fourth(ref, first):
-        return jnp.concatenate([ref[pl.ds(first + 4 * k, 1), :] for k in range(4)], axis=0)
 
     def pass_on():
         landed(rrecv, rlr).wait()
@@ -324,8 +319,7 @@
             for m in range(2):
                 buf = msg.at[2 * 4 + ro * 2 + m]
                 put(src, ro, m, past, buf)
-                extra = jnp.concatenate([every_fourth(rrecv, kind * 16 + 2 * m + k) for k in range(2)], axis=0)
-                buf[...] = buf[...] + extra
+                buf[...] = buf[...] + rrecv[(kind * 2 + m) * 8:(kind * 2 + m + 1) * 8, :]
                 copy(2, ro, m, past).start()
 
     landed(tg.at[pl.ds(0, 3), pl.ds(0, n)], gr.at[5]).wait()
@@ -347,6 +341,22 @@
         part[s, :, :] = (jnp.dot(tg[2 * r], va[...], preferred_element_type=F32)
                          + jnp.dot(tg[2 * r + 1], vb[...], preferred_element_type=F32))
         ladder_copy(s).start()
+
+        @pl.when(s == 0)
+        def _():
+            send(s4, smsg, s_copy, 1, ro, via)
+
+        @pl.when(s == 1)
+        def _():
+            send(s4, smsg, s_copy, 1, di, via)
+
+        @pl.when(s == 2)
+        def _():
+            send(st4, pmsg, p_copy, 1, ro, via)
+
+        @pl.when(jnp.logical_and(s == 3, home == 0))
+        def _():
+            send(st4, pmsg, p_copy, 1, di, via)
 
         @pl.when(s == 5)
         def _():
@@ -377,13 +387,11 @@
 
     landed(rmsg, rls).wait()
     landed(srecv.at[pl.ds(0, 80)], srs).wait()
-    @pl.loop(0, 8)
-    def _(i):
+    for i in range(8):
         for jh in range(2):
-            line = pl.ds(pl.multiple_of(i * 16 + jh * 8, 8), 8)
-            sv = jnp.concatenate(
-                [every_fourth(srecv, ((2 * jh + cc) * 2 + i // 4) * 16 + i % 4) for cc in range(2)], axis=0)
-            out_ref[line, :] = out_ref[line, :] + sv
+            line = slice(i * 16 + jh * 8, i * 16 + jh * 8 + 8)
+            rows4 = [((2 * jh + cc) * 4 + i // 2) * 8 + i % 2 * 4 for cc in range(2)]
+            out_ref[line, :] = out_ref[line, :] + jnp.concatenate([srecv[k:k + 4, :] for k in rows4], axis=0)
 
     @pl.when(home == 1)
     def _():

time: 51.2 us -> 49.9 us (0.975)
  Pallas kernels: 49.9 us -> 48.6 us
    pallas_call x1, Pallas kernels: 49.9 us -> 48.6 us  [sweep(): pl.pallas_call(sweep_kernel, out_shape=jax.ShapeDtypeStruct((n, w), F32),...]
where the time goes in v7:
time: 49.9 us; the launch traced here: 49.8 us
  Pallas kernels  48.6 us (97%)
  other arithmetic  1.17 us (2%)
    pallas_call x1, Pallas kernels, sweep(): pl.pallas_call(sweep_kernel, out_shape=jax.ShapeDtypeStruct((n, w), F32),...  48.6 us
    div x1, other arithmetic, local_sweep(): return sweep(t_blk, oovv_blk, vvvv_blk, oooo_full, wd_blk, wx_blk) / d_blk  1.17 us

profile of v7, /device:TPU:0, one launch (start us, length us, event | category | flops | bytes accessed | tf_op | source)
XLA Modules:
  0.0 49.8 jit_solution(6424804113102094446)
XLA Ops:
  0.0 0.0 copy-start
  0.0 48.6 %sweep.1 = f32[128,2304]{1,0:T(8,128)S(1)} custom-call(f32[128,2304]{1,0:T(8,128)} %t_hbm.1, bf16[128,2304]{1,0:T(8,128)(2,1)} %oovv_hbm.1, bf16[4608,2304]{1,0:T(8,128)(2,1)} %v_hbm.1, bf16[256,256]{1,0:T(8,128)(2,1)} %oooo_hbm.1, bf16[1536,384]{1,0:T(8,128)(2,1)} %wd_hbm.1, bf16[1536,384]{1,0:T(8,128)(2,1)} %wx_hbm.1), custom_call_target="tpu_custom_call" | custom-call | tf_op jit(solution)/shard_map/sweep/pallas_call | solution.py:432
  48.6 0.0 copy-done
  48.6 1.2 %div.3 = f32[128,2304]{1,0:T(8,128)} divide(f32[128,2304]{1,0:T(8,128)S(1)} %sweep.1, f32[128,2304]{1,0:T(8,128)S(1)} %copy-done) | non-fusion elementwise | flops 294912 | bytes 3538944 | tf_op jit(solution)/shard_map/div | solution.py:456
Async XLA Ops:
  0.0 48.6 %copy-start = (f32[128,2304]{1,0:T(8,128)S(1)}, f32[128,2304]{1,0:T(8,128)}, u32[]{:S(2)}) copy-start(f32[128,2304]{1,0:T(8,128)} %param.8) | copy-start | bytes 3538948

commit v8 on v7

--- a/solution.py
+++ b/solution.py
@@ -205,6 +205,65 @@
     direct(ny)
     exchange((c, nx, ny), 0)
 
+    def s_rows(i, j):
+        return pl.ds(pl.multiple_of((i * 4 + j) * PITCH, 8), VIRT)
+
+    def t_rows(i, j):
+        return pl.ds(pl.multiple_of(((i // 4) * 16 + j * 4 + i % 4) * PITCH, 8), VIRT)
+
+    def block(i, j):
+        direct_part = jnp.concatenate(
+            [ubuf[chip, pl.ds(pl.multiple_of(i * 24, 8), 24), pl.ds(pl.multiple_of(j * LANE, LANE), LANE)]
+             for chip in range(4)], axis=0)
+        return direct_part - vbuf_s[
+            i // 2, pl.ds(pl.multiple_of(j * VIRT, 8), VIRT), pl.ds(pl.multiple_of((i % 2) * LANE, LANE), LANE)]
+
+    def fill_s(ih):
+        @pl.loop(0, 4)
+        def _(j):
+            for e in range(4):
+                s4[s_rows(ih * 4 + e, j), :] = block(ih * 4 + e, j)
+
+    def fill_t(ih):
+        @pl.loop(0, 4)
+        def _(j):
+            for e in range(4):
+                st4[t_rows(ih * 4 + e, j), :VIRT] = s4[s_rows(ih * 4 + e, j), :].T[:VIRT, :]
+
+    def put(src, ih, m, chip, dst):
+        first = (ih * 16 + m * 8) * PITCH + chip * 24
+        for g in range(6):
+            vals = [src[pl.ds(first + g * 4 + e, 8, stride=PITCH), :][:, :VIRT] for e in range(4)]
+            dst[:, g * 384:(g + 1) * 384] = jnp.concatenate(vals, axis=1)
+
+    def s_copy(slot, ih, m, chip):
+        buf = smsg.at[slot * 4 + ih * 2 + m]
+        return _rcopy(buf, srecv.at[slot_s(c, ih, m)], ss, srs, _dev(chip, r))
+
+    def p_copy(slot, ih, m, chip):
+        buf = pmsg.at[slot * 4 + ih * 2 + m]
+        return _rcopy(buf, precv.at[slot_p(1 - home, half, ih, m)], ps, prs, _dev(chip, own))
+
+    def relay(kind, src):
+        @pl.loop(0, 2)
+        def _(m):
+            put(src, ro, m, dg, rmsg.at[kind * 2 + m])
+            to = rrecv.at[pl.ds(pl.multiple_of((kind * 2 + m) * 8, 8), 8)]
+            _rcopy(rmsg.at[kind * 2 + m], to, rls, rlr, _dev(via, own)).start()
+
+    def send(src, msg, copy, slot, ih, chip):
+        @pl.loop(0, 2)
+        def _(m):
+            put(src, ih, m, chip, msg.at[slot * 4 + ih * 2 + m])
+            copy(slot, ih, m, chip).start()
+
+    def mirror():
+        @pl.loop(0, 4)
+        def _(j):
+            for e in range(4):
+                at = s_rows(half * 4 + e, j)
+                s4[at, :VIRT] = s4[at, :VIRT] + block(half * 4 + j, e).T[:VIRT, :]
+
     @pl.loop(0, 4)
     def _(p):
         landed(tg.at[dg, pl.ds(0, n // 4)], fr.at[p]).wait()
@@ -213,63 +272,31 @@
         ubuf[dg, pl.ds(pl.multiple_of(p * 48, 16), 48), :] = direct_rows(dg, 2 * p, 2)
         exchange_pair((dg,), 3, p)
 
+        @pl.when(p == 1)
+        def _():
+            fill_s(0)
+
+            @pl.when(ro == 0)
+            def _():
+                relay(0, s4)
+
+            @pl.when(ro == 1)
+            def _():
+                @pl.when(home == 1)
+                def _():
+                    mirror()
+
+                send(s4, smsg, s_copy, 1, 0, via)
+
     d_d = tcopy(dg, whole, 5, _dev(c, o))
     d_d.start()
 
-    def s_rows(i, j):
-        return pl.ds(pl.multiple_of((i * 4 + j) * PITCH, 8), VIRT)
-
-    def t_rows(i, j):
-        return pl.ds(pl.multiple_of(((i // 4) * 16 + j * 4 + i % 4) * PITCH, 8), VIRT)
-
-    def block(i, j):
-        direct_part = jnp.concatenate(
-            [ubuf[chip, pl.ds(pl.multiple_of(i * 24, 8), 24), pl.ds(pl.multiple_of(j * LANE, LANE), LANE)]
-             for chip in range(4)], axis=0)
-        return direct_part - vbuf_s[
-            i // 2, pl.ds(pl.multiple_of(j * VIRT, 8), VIRT), pl.ds(pl.multiple_of((i % 2) * LANE, LANE), LANE)]
-
-    def fill_s(ih):
-        @pl.loop(0, 4)
-        def _(j):
-            for e in range(4):
-                s4[s_rows(ih * 4 + e, j), :] = block(ih * 4 + e, j)
-
-    def fill_t(ih):
-        @pl.loop(0, 4)
-        def _(j):
-            for e in range(4):
-                st4[t_rows(ih * 4 + e, j), :VIRT] = s4[s_rows(ih * 4 + e, j), :].T[:VIRT, :]
-
-    def put(src, ih, m, chip, dst):
-        first = (ih * 16 + m * 8) * PITCH + chip * 24
-        for g in range(6):
-            vals = [src[pl.ds(first + g * 4 + e, 8, stride=PITCH), :][:, :VIRT] for e in range(4)]
-            dst[:, g * 384:(g + 1) * 384] = jnp.concatenate(vals, axis=1)
-
-    def s_copy(slot, ih, m, chip):
-        buf = smsg.at[slot * 4 + ih * 2 + m]
-        return _rcopy(buf, srecv.at[slot_s(c, ih, m)], ss, srs, _dev(chip, r))
-
-    def p_copy(slot, ih, m, chip):
-        buf = pmsg.at[slot * 4 + ih * 2 + m]
-        return _rcopy(buf, precv.at[slot_p(1 - home, half, ih, m)], ps, prs, _dev(chip, own))
-
-    def relay(kind, src):
-        @pl.loop(0, 2)
-        def _(m):
-            put(src, ro, m, dg, rmsg.at[kind * 2 + m])
-            to = rrecv.at[pl.ds(pl.multiple_of((kind * 2 + m) * 8, 8), 8)]
-            _rcopy(rmsg.at[kind * 2 + m], to, rls, rlr, _dev(via, own)).start()
-
-    def send(src, msg, copy, slot, ih, chip):
-        @pl.loop(0, 2)
-        def _(m):
-            put(src, ih, m, chip, msg.at[slot * 4 + ih * 2 + m])
-            copy(slot, ih, m, chip).start()
-
-    fill_s(ro)
-    relay(0, s4)
+    fill_s(1)
+
+    @pl.when(ro == 1)
+    def _():
+        relay(0, s4)
+
     fill_t(ro)
     relay(1, st4)
 
@@ -281,15 +308,9 @@
         part_m = mfull.at[krows, pl.ds(pl.multiple_of(rr * n, n), n)]
         _rcopy(part_m, part_m, ms, mrs, _dev(cc, rr)).start()
 
-    fill_s(di)
-
-    @pl.when(home == 1)
-    def _():
-        @pl.loop(0, 4)
-        def _(j):
-            for e in range(4):
-                at = s_rows(half * 4 + e, j)
-                s4[at, :VIRT] = s4[at, :VIRT] + block(half * 4 + j, e).T[:VIRT, :]
+    @pl.when(jnp.logical_and(home == 1, di == 1))
+    def _():
+        mirror()
 
     send(s4, smsg, s_copy, 2, di, past)
     send(s4, smsg, s_copy, 0, di, dg)
@@ -346,9 +367,9 @@
         def _():
             send(s4, smsg, s_copy, 1, ro, via)
 
-        @pl.when(s == 1)
-        def _():
-            send(s4, smsg, s_copy, 1, di, via)
+        @pl.when(jnp.logical_and(s == 1, di == 1))
+        def _():
+            send(s4, smsg, s_copy, 1, 1, via)
 
         @pl.when(s == 2)
         def _():

time: 49.9 us -> 49.4 us (0.990)
  Pallas kernels: 48.6 us -> 48.1 us
    pallas_call x1, Pallas kernels: 48.6 us -> 48.1 us  [sweep(): pl.pallas_call(sweep_kernel, out_shape=jax.ShapeDtypeStruct((n, w), F32),...]
where the time goes in v8:
time: 49.4 us; the launch traced here: 49.3 us
  Pallas kernels  48.1 us (97%)
  other arithmetic  1.17 us (2%)
    pallas_call x1, Pallas kernels, sweep(): pl.pallas_call(sweep_kernel, out_shape=jax.ShapeDtypeStruct((n, w), F32),...  48.1 us
    div x1, other arithmetic, local_sweep(): return sweep(t_blk, oovv_blk, vvvv_blk, oooo_full, wd_blk, wx_blk) / d_blk  1.17 us

profile of v8, /device:TPU:0, one launch (start us, length us, event | category | flops | bytes accessed | tf_op | source)
XLA Modules:
  0.0 49.3 jit_solution(3724847868354007695)
XLA Ops:
  0.0 0.0 copy-start
  0.0 48.1 %sweep.1 = f32[128,2304]{1,0:T(8,128)S(1)} custom-call(f32[128,2304]{1,0:T(8,128)} %t_hbm.1, bf16[128,2304]{1,0:T(8,128)(2,1)} %oovv_hbm.1, bf16[4608,2304]{1,0:T(8,128)(2,1)} %v_hbm.1, bf16[256,256]{1,0:T(8,128)(2,1)} %oooo_hbm.1, bf16[1536,384]{1,0:T(8,128)(2,1)} %wd_hbm.1, bf16[1536,384]{1,0:T(8,128)(2,1)} %wx_hbm.1), custom_call_target="tpu_custom_call" | custom-call | tf_op jit(solution)/shard_map/sweep/pallas_call | solution.py:453
  48.1 0.0 copy-done
  48.1 1.2 %div.3 = f32[128,2304]{1,0:T(8,128)} divide(f32[128,2304]{1,0:T(8,128)S(1)} %sweep.1, f32[128,2304]{1,0:T(8,128)S(1)} %copy-done) | non-fusion elementwise | flops 294912 | bytes 3538944 | tf_op jit(solution)/shard_map/div | solution.py:477
Async XLA Ops:
  0.0 48.1 %copy-start = (f32[128,2304]{1,0:T(8,128)S(1)}, f32[128,2304]{1,0:T(8,128)}, u32[]{:S(2)}) copy-start(f32[128,2304]{1,0:T(8,128)} %param.8) | copy-start | bytes 3538948

commit v9 on v8

--- a/solution.py
+++ b/solution.py
@@ -48,8 +48,6 @@
     oload = pltpu.make_async_copy(oovv_hbm, oovv, lsem.at[4])
     hload = pltpu.make_async_copy(oooo_hbm, oooo, lsem.at[5])
     wloads = [pltpu.make_async_copy(a, ww.at[k], lsem.at[6]) for k, a in enumerate((wd_hbm, wx_hbm))]
-    for cp in (*wloads, oload, hload):
-        cp.start()
 
     own = c // 2
     half = c % 2
@@ -84,9 +82,16 @@
 
     for k in range(4):
         tloads[k].wait()
-        tg[c, pl.ds(pl.multiple_of(r * n + k * chunk, chunk), chunk), :] = t32[k * chunk:(k + 1) * chunk, :].astype(BF16)
-
-    pl.semaphore_wait(sem, 7)
+        part_t = pl.ds(pl.multiple_of(r * n + k * chunk, chunk), chunk)
+        tg[c, part_t, :] = t32[k * chunk:(k + 1) * chunk, :].astype(BF16)
+        if k == 0:
+            pl.semaphore_wait(sem, 7)
+        for lanes, g, chip in ((h0, 1, nx), (h1, 2, ny)):
+            ref = tg.at[c, part_t, lanes]
+            _rcopy(ref, ref, gs, gr.at[g], _dev(chip, r)).start()
+
+    for cp in (*wloads, oload, hload):
+        cp.start()
 
     def tcopy(chip, lanes, k, dev):
         ref = tg.at[chip, rows, lanes]
@@ -102,8 +107,6 @@
     d_own = tcopy(c, whole, 0, _dev(c, o))
     x1 = tcopy(c, h1, 3, _dev(nx, r))
     y0 = tcopy(c, h0, 4, _dev(ny, r))
-    x0.start()
-    y1.start()
     d_own.start()
     x1.start()
     y0.start()
@@ -312,14 +315,38 @@
     def _():
         mirror()
 
-    send(s4, smsg, s_copy, 2, di, past)
-    send(s4, smsg, s_copy, 0, di, dg)
+    early = via == 0
+    late = jnp.logical_not(early)
 
     @pl.when(home == 0)
     def _():
         fill_t(di)
-        send(st4, pmsg, p_copy, 2, di, past)
-        send(st4, pmsg, p_copy, 0, di, dg)
+
+    @pl.when(early)
+    def _():
+        send(s4, smsg, s_copy, 1, ro, via)
+        send(st4, pmsg, p_copy, 1, ro, via)
+
+        @pl.when(di == 1)
+        def _():
+            send(s4, smsg, s_copy, 1, 1, via)
+
+        @pl.when(home == 0)
+        def _():
+            send(st4, pmsg, p_copy, 1, di, via)
+
+    @pl.when(late)
+    def _():
+        send(s4, smsg, s_copy, 0, di, dg)
+        send(s4, smsg, s_copy, 2, di, past)
+
+        @pl.when(home == 0)
+        def _():
+            send(st4, pmsg, p_copy, 0, di, dg)
+            send(st4, pmsg, p_copy, 2, di, past)
+
+    @pl.when(home == 0)
+    def _():
         send(st4, pmsg, p_copy, 3, ro, c)
         send(st4, pmsg, p_copy, 3, di, c)
 
@@ -363,21 +390,31 @@
                          + jnp.dot(tg[2 * r + 1], vb[...], preferred_element_type=F32))
         ladder_copy(s).start()
 
-        @pl.when(s == 0)
+        @pl.when(jnp.logical_and(s == 0, late))
         def _():
             send(s4, smsg, s_copy, 1, ro, via)
 
-        @pl.when(jnp.logical_and(s == 1, di == 1))
+        @pl.when(jnp.logical_and(s == 1, jnp.logical_and(late, di == 1)))
         def _():
             send(s4, smsg, s_copy, 1, 1, via)
 
-        @pl.when(s == 2)
+        @pl.when(jnp.logical_and(s == 2, late))
         def _():
             send(st4, pmsg, p_copy, 1, ro, via)
 
-        @pl.when(jnp.logical_and(s == 3, home == 0))
+        @pl.when(jnp.logical_and(s == 3, jnp.logical_and(late, home == 0)))
         def _():
             send(st4, pmsg, p_copy, 1, di, via)
+
+        @pl.when(jnp.logical_and(s == 0, early))
+        def _():
+            send(s4, smsg, s_copy, 2, di, past)
+            send(s4, smsg, s_copy, 0, di, dg)
+
+        @pl.when(jnp.logical_and(s == 1, jnp.logical_and(early, home == 0)))
+        def _():
+            send(st4, pmsg, p_copy, 2, di, past)
+            send(st4, pmsg, p_copy, 0, di, dg)
 
         @pl.when(s == 5)
         def _():

time: 49.4 us -> 49.4 us (level)
  no operation moved by 1% of the time
where the time goes in v9:
time: 49.4 us; the launch traced here: 49.2 us
  Pallas kernels  48 us (97%)
  other arithmetic  1.17 us (2%)
    pallas_call x1, Pallas kernels, sweep(): pl.pallas_call(sweep_kernel, out_shape=jax.ShapeDtypeStruct((n, w), F32),...  48 us
    div x1, other arithmetic, local_sweep(): return sweep(t_blk, oovv_blk, vvvv_blk, oooo_full, wd_blk, wx_blk) / d_blk  1.17 us

profile of v9, /device:TPU:0, one launch (start us, length us, event | category | flops | bytes accessed | tf_op | source)
XLA Modules:
  0.0 49.2 jit_solution(4298055326055846633)
XLA Ops:
  0.0 0.0 copy-start
  0.0 48.0 %sweep.1 = f32[128,2304]{1,0:T(8,128)S(1)} custom-call(f32[128,2304]{1,0:T(8,128)} %t_hbm.1, bf16[128,2304]{1,0:T(8,128)(2,1)} %oovv_hbm.1, bf16[4608,2304]{1,0:T(8,128)(2,1)} %v_hbm.1, bf16[256,256]{1,0:T(8,128)(2,1)} %oooo_hbm.1, bf16[1536,384]{1,0:T(8,128)(2,1)} %wd_hbm.1, bf16[1536,384]{1,0:T(8,128)(2,1)} %wx_hbm.1), custom_call_target="tpu_custom_call" | custom-call | tf_op jit(solution)/shard_map/sweep/pallas_call | solution.py:490
  48.1 0.0 copy-done
  48.1 1.2 %div.3 = f32[128,2304]{1,0:T(8,128)} divide(f32[128,2304]{1,0:T(8,128)S(1)} %sweep.1, f32[128,2304]{1,0:T(8,128)S(1)} %copy-done) | non-fusion elementwise | flops 294912 | bytes 3538944 | tf_op jit(solution)/shard_map/div | solution.py:514
Async XLA Ops:
  0.0 48.1 %copy-start = (f32[128,2304]{1,0:T(8,128)S(1)}, f32[128,2304]{1,0:T(8,128)}, u32[]{:S(2)}) copy-start(f32[128,2304]{1,0:T(8,128)} %param.8) | copy-start | bytes 3538948

commit v10 on v8

--- a/solution.py
+++ b/solution.py
@@ -48,8 +48,6 @@
     oload = pltpu.make_async_copy(oovv_hbm, oovv, lsem.at[4])
     hload = pltpu.make_async_copy(oooo_hbm, oooo, lsem.at[5])
     wloads = [pltpu.make_async_copy(a, ww.at[k], lsem.at[6]) for k, a in enumerate((wd_hbm, wx_hbm))]
-    for cp in (*wloads, oload, hload):
-        cp.start()
 
     own = c // 2
     half = c % 2
@@ -59,17 +57,17 @@
     ro = (home + half) % 2
     di = 1 - ro
 
-    def slot_s(chip, ih, m):
-        return pl.ds(pl.multiple_of(((chip * 2 + ih) * 2 + m) * 8, 8), 8)
-
-    def slot_p(kind, a, ih, m):
-        return ((kind * 2 + a) * 2 + ih) * 2 + m
+    def slot_s(chip, ih):
+        return (chip * 2 + ih) * 2
+
+    def slot_p(kind, a, ih):
+        return ((kind * 2 + a) * 2 + ih) * 2
 
     zero8 = jnp.zeros((8, w), F32)
     for m in range(2):
-        srecv[slot_s(dg, ro, m), :] = zero8
-        precv[slot_p(0, 1 - half, half, m)] = zero8
-        precv[slot_p(1, 1 - half, 1 - half, m)] = zero8
+        srecv[slot_s(dg, ro) + m] = zero8
+        precv[slot_p(0, 1 - half, half) + m] = zero8
+        precv[slot_p(1, 1 - half, 1 - half) + m] = zero8
 
     sem = pltpu.get_barrier_semaphore()
     for cc, rr in ((nx, r), (ny, r), (dg, r), (c, o), (nx, o), (ny, o), (dg, o)):
@@ -84,9 +82,16 @@
 
     for k in range(4):
         tloads[k].wait()
-        tg[c, pl.ds(pl.multiple_of(r * n + k * chunk, chunk), chunk), :] = t32[k * chunk:(k + 1) * chunk, :].astype(BF16)
-
-    pl.semaphore_wait(sem, 7)
+        part_t = pl.ds(pl.multiple_of(r * n + k * chunk, chunk), chunk)
+        tg[c, part_t, :] = t32[k * chunk:(k + 1) * chunk, :].astype(BF16)
+        if k == 0:
+            pl.semaphore_wait(sem, 7)
+        for lanes, g, chip in ((h0, 1, nx), (h1, 2, ny)):
+            ref = tg.at[c, part_t, lanes]
+            _rcopy(ref, ref, gs, gr.at[g], _dev(chip, r)).start()
+
+    for cp in (*wloads, oload, hload):
+        cp.start()
 
     def tcopy(chip, lanes, k, dev):
         ref = tg.at[chip, rows, lanes]
@@ -102,8 +107,6 @@
     d_own = tcopy(c, whole, 0, _dev(c, o))
     x1 = tcopy(c, h1, 3, _dev(nx, r))
     y0 = tcopy(c, h0, 4, _dev(ny, r))
-    x0.start()
-    y1.start()
     d_own.start()
     x1.start()
     y0.start()
@@ -236,26 +239,28 @@
             vals = [src[pl.ds(first + g * 4 + e, 8, stride=PITCH), :][:, :VIRT] for e in range(4)]
             dst[:, g * 384:(g + 1) * 384] = jnp.concatenate(vals, axis=1)
 
-    def s_copy(slot, ih, m, chip):
-        buf = smsg.at[slot * 4 + ih * 2 + m]
-        return _rcopy(buf, srecv.at[slot_s(c, ih, m)], ss, srs, _dev(chip, r))
-
-    def p_copy(slot, ih, m, chip):
-        buf = pmsg.at[slot * 4 + ih * 2 + m]
-        return _rcopy(buf, precv.at[slot_p(1 - home, half, ih, m)], ps, prs, _dev(chip, own))
+    def s_copy(slot, ih, chip):
+        buf = smsg.at[pl.ds(slot * 4 + ih * 2, 2)]
+        return _rcopy(buf, srecv.at[pl.ds(slot_s(c, ih), 2)], ss, srs, _dev(chip, r))
+
+    def p_copy(slot, ih, chip):
+        buf = pmsg.at[pl.ds(slot * 4 + ih * 2, 2)]
+        return _rcopy(buf, precv.at[pl.ds(slot_p(1 - home, half, ih), 2)], ps, prs, _dev(chip, own))
 
     def relay(kind, src):
         @pl.loop(0, 2)
         def _(m):
             put(src, ro, m, dg, rmsg.at[kind * 2 + m])
-            to = rrecv.at[pl.ds(pl.multiple_of((kind * 2 + m) * 8, 8), 8)]
-            _rcopy(rmsg.at[kind * 2 + m], to, rls, rlr, _dev(via, own)).start()
+
+        pair = pl.ds(kind * 2, 2)
+        _rcopy(rmsg.at[pair], rrecv.at[pair], rls, rlr, _dev(via, own)).start()
 
     def send(src, msg, copy, slot, ih, chip):
         @pl.loop(0, 2)
         def _(m):
             put(src, ih, m, chip, msg.at[slot * 4 + ih * 2 + m])
-            copy(slot, ih, m, chip).start()
+
+        copy(slot, ih, chip).start()
 
     def mirror():
         @pl.loop(0, 4)
@@ -326,13 +331,13 @@
     @pl.loop(0, 2)
     def _(m):
         for ih in range(2):
-            put(s4, ih, m, c, srecv.at[slot_s(c, ih, m)])
+            put(s4, ih, m, c, srecv.at[slot_s(c, ih) + m])
 
     @pl.when(home == 1)
     def _():
         @pl.loop(0, 2)
         def _(m):
-            put(st4, ro, m, c, precv.at[slot_p(0, half, ro, m)])
+            put(st4, ro, m, c, precv.at[slot_p(0, half, ro) + m])
 
     def pass_on():
         landed(rrecv, rlr).wait()
@@ -340,8 +345,8 @@
             for m in range(2):
                 buf = msg.at[2 * 4 + ro * 2 + m]
                 put(src, ro, m, past, buf)
-                buf[...] = buf[...] + rrecv[(kind * 2 + m) * 8:(kind * 2 + m + 1) * 8, :]
-                copy(2, ro, m, past).start()
+                buf[...] = buf[...] + rrecv[kind * 2 + m]
+            copy(2, ro, past).start()
 
     landed(tg.at[pl.ds(0, 3), pl.ds(0, n)], gr.at[5]).wait()
 
@@ -407,12 +412,13 @@
         out_ref[line, :] = oovv[line, :].astype(F32) + (mine + theirs[line, :] + hole[line, :])
 
     landed(rmsg, rls).wait()
-    landed(srecv.at[pl.ds(0, 80)], srs).wait()
+    landed(srecv.at[pl.ds(0, 10)], srs).wait()
     for i in range(8):
         for jh in range(2):
             line = slice(i * 16 + jh * 8, i * 16 + jh * 8 + 8)
-            rows4 = [((2 * jh + cc) * 4 + i // 2) * 8 + i % 2 * 4 for cc in range(2)]
-            out_ref[line, :] = out_ref[line, :] + jnp.concatenate([srecv[k:k + 4, :] for k in rows4], axis=0)
+            rows4 = slice(i % 2 * 4, i % 2 * 4 + 4)
+            both = [srecv[(2 * jh + cc) * 4 + i // 2, rows4, :] for cc in range(2)]
+            out_ref[line, :] = out_ref[line, :] + jnp.concatenate(both, axis=0)
 
     @pl.when(home == 1)
     def _():
@@ -428,7 +434,7 @@
             m, rows4 = j // 2, slice(j % 2 * 4, j % 2 * 4 + 4)
             for kind, row in ((0, r), (1, o)):
                 line = pl.ds(pl.multiple_of((a * 4 + j) * 16 + row * 8, 8), 8)
-                both = [zero4 if kind == 0 and ih == a else precv[slot_p(kind, a, ih, m), rows4, :] for ih in range(2)]
+                both = [zero4 if kind == 0 and ih == a else precv[slot_p(kind, a, ih) + m, rows4, :] for ih in range(2)]
                 out_ref[line, :] = out_ref[line, :] + jnp.concatenate(both, axis=0)
 
     landed(smsg.at[pl.ds(0, 10)], ss).wait()
@@ -462,7 +468,7 @@
             V((n * PITCH, LANE), F32), V((OCC * LANE, 4 * LANE), BF16), V((wx.shape[1], wx.shape[0]), BF16),
             V((4, 2 * VIRT, 4 * LANE), F32), V((4, 4 * VIRT, 2 * LANE), F32),
             V((32 * PITCH, LANE), F32), V((32 * PITCH, LANE), F32),
-            V((12, 8, w), F32), V((16, 8, w), F32), V((128, w), F32), V((16, 8, w), F32), V((4, 8, w), F32), V((32, w), F32),
+            V((12, 8, w), F32), V((16, 8, w), F32), V((16, 8, w), F32), V((16, 8, w), F32), V((4, 8, w), F32), V((4, 8, w), F32),
             V((3, depth, STEP), BF16), V((n, w), F32), V((w // STEP, 2 * n, STEP), F32), V(wx.shape, F32),
             DMA((7,)), DMA, DMA((6,)), DMA, DMA((4,)), DMA, DMA, DMA, DMA,
             DMA, DMA, DMA, DMA, DMA, DMA, DMA((3,)), DMA, DMA,

time: 49.4 us -> 49.5 us (level)
  no operation moved by 1% of the time
where the time goes in v10:
time: 49.5 us; the launch traced here: 49.3 us
  Pallas kernels  48.1 us (97%)
  other arithmetic  1.17 us (2%)
    pallas_call x1, Pallas kernels, sweep(): pl.pallas_call(sweep_kernel, out_shape=jax.ShapeDtypeStruct((n, w), F32),...  48.1 us
    div x1, other arithmetic, local_sweep(): return sweep(t_blk, oovv_blk, vvvv_blk, oooo_full, wd_blk, wx_blk) / d_blk  1.17 us

profile of v10, /device:TPU:0, one launch (start us, length us, event | category | flops | bytes accessed | tf_op | source)
XLA Modules:
  0.0 49.3 jit_solution(6523188978450405486)
XLA Ops:
  0.0 0.0 copy-start
  0.0 48.1 %sweep.1 = f32[128,2304]{1,0:T(8,128)S(1)} custom-call(f32[128,2304]{1,0:T(8,128)} %t_hbm.1, bf16[128,2304]{1,0:T(8,128)(2,1)} %oovv_hbm.1, bf16[4608,2304]{1,0:T(8,128)(2,1)} %v_hbm.1, bf16[256,256]{1,0:T(8,128)(2,1)} %oooo_hbm.1, bf16[1536,384]{1,0:T(8,128)(2,1)} %wd_hbm.1, bf16[1536,384]{1,0:T(8,128)(2,1)} %wx_hbm.1), custom_call_target="tpu_custom_call" | custom-call | tf_op jit(solution)/shard_map/sweep/pallas_call | solution.py:459
  48.1 0.0 copy-done
  48.2 1.2 %div.3 = f32[128,2304]{1,0:T(8,128)} divide(f32[128,2304]{1,0:T(8,128)S(1)} %sweep.1, f32[128,2304]{1,0:T(8,128)S(1)} %copy-done) | non-fusion elementwise | flops 294912 | bytes 3538944 | tf_op jit(solution)/shard_map/div | solution.py:483
Async XLA Ops:
  0.0 48.1 %copy-start = (f32[128,2304]{1,0:T(8,128)S(1)}, f32[128,2304]{1,0:T(8,128)}, u32[]{:S(2)}) copy-start(f32[128,2304]{1,0:T(8,128)} %param.8) | copy-start | bytes 3538948

commit v11 on v8

--- a/solution.py
+++ b/solution.py
@@ -40,6 +40,10 @@
     rows = pl.ds(pl.multiple_of(r * n, n), n)
     orows = pl.ds(pl.multiple_of(o * n, n), n)
 
+    sem = pltpu.get_barrier_semaphore()
+    for cc, rr in ((nx, r), (ny, r), (dg, r), (c, o), (nx, o), (ny, o), (dg, o)):
+        pl.semaphore_signal(sem, inc=1, device_id=_dev(cc, rr), device_id_type=MESH)
+
     chunk = n // 4
     tloads = [pltpu.make_async_copy(t_hbm.at[pl.ds(k * chunk, chunk)], t32.at[pl.ds(k * chunk, chunk)], lsem.at[k])
               for k in range(4)]
@@ -64,16 +68,6 @@
 
     def slot_p(kind, a, ih, m):
         return ((kind * 2 + a) * 2 + ih) * 2 + m
-
-    zero8 = jnp.zeros((8, w), F32)
-    for m in range(2):
-        srecv[slot_s(dg, ro, m), :] = zero8
-        precv[slot_p(0, 1 - half, half, m)] = zero8
-        precv[slot_p(1, 1 - half, 1 - half, m)] = zero8
-
-    sem = pltpu.get_barrier_semaphore()
-    for cc, rr in ((nx, r), (ny, r), (dg, r), (c, o), (nx, o), (ny, o), (dg, o)):
-        pl.semaphore_signal(sem, inc=1, device_id=_dev(cc, rr), device_id_type=MESH)
 
     def vcopy(s, slot):
         lanes = pl.ds(pl.multiple_of(s * STEP, STEP), STEP)
@@ -124,6 +118,16 @@
         @pl.loop(0, n // 16)
         def _(ib):
             spread_rows(chip, ib, first, groups)
+
+    zero8 = jnp.zeros((8, w), F32)
+    for m in range(2):
+        srecv[slot_s(dg, ro, m), :] = zero8
+
+    @pl.when(home == 0)
+    def _():
+        for m in range(2):
+            precv[slot_p(0, 1 - half, half, m)] = zero8
+            precv[slot_p(1, 1 - half, 1 - half, m)] = zero8
 
     spread(c, 0, 6)
 
@@ -276,17 +280,17 @@
         def _():
             fill_s(0)
 
-            @pl.when(ro == 0)
+            @pl.when(jnp.logical_and(home == 1, ro == 1))
             def _():
-                relay(0, s4)
-
-            @pl.when(ro == 1)
-            def _():
-                @pl.when(home == 1)
-                def _():
-                    mirror()
-
-                send(s4, smsg, s_copy, 1, 0, via)
+                mirror()
+
+        @pl.when(jnp.logical_and(p == 2, ro == 0))
+        def _():
+            relay(0, s4)
+
+        @pl.when(jnp.logical_and(p == 2, ro == 1))
+        def _():
+            send(s4, smsg, s_copy, 1, 0, via)
 
     d_d = tcopy(dg, whole, 5, _dev(c, o))
     d_d.start()

time: 49.4 us -> 50 us (1.012)
  Pallas kernels: 48.1 us -> 48.7 us
    pallas_call x1, Pallas kernels: 48.1 us -> 48.7 us  [sweep(): pl.pallas_call(sweep_kernel, out_shape=jax.ShapeDtypeStruct((n, w), F32),...]
where the time goes in v11:
time: 50 us; the launch traced here: 49.9 us
  Pallas kernels  48.7 us (97%)
  other arithmetic  1.17 us (2%)
    pallas_call x1, Pallas kernels, sweep(): pl.pallas_call(sweep_kernel, out_shape=jax.ShapeDtypeStruct((n, w), F32),...  48.7 us
    div x1, other arithmetic, local_sweep(): return sweep(t_blk, oovv_blk, vvvv_blk, oooo_full, wd_blk, wx_blk) / d_blk  1.17 us

profile of v11, /device:TPU:0, one launch (start us, length us, event | category | flops | bytes accessed | tf_op | source)
XLA Modules:
  0.0 49.9 jit_solution(17869065577105951125)
XLA Ops:
  0.0 0.0 copy-start
  0.0 48.7 %sweep.1 = f32[128,2304]{1,0:T(8,128)S(1)} custom-call(f32[128,2304]{1,0:T(8,128)} %t_hbm.1, bf16[128,2304]{1,0:T(8,128)(2,1)} %oovv_hbm.1, bf16[4608,2304]{1,0:T(8,128)(2,1)} %v_hbm.1, bf16[256,256]{1,0:T(8,128)(2,1)} %oooo_hbm.1, bf16[1536,384]{1,0:T(8,128)(2,1)} %wd_hbm.1, bf16[1536,384]{1,0:T(8,128)(2,1)} %wx_hbm.1), custom_call_target="tpu_custom_call" | custom-call | tf_op jit(solution)/shard_map/sweep/pallas_call | solution.py:457
  48.7 0.0 copy-done
  48.7 1.2 %div.3 = f32[128,2304]{1,0:T(8,128)} divide(f32[128,2304]{1,0:T(8,128)S(1)} %sweep.1, f32[128,2304]{1,0:T(8,128)S(1)} %copy-done) | non-fusion elementwise | flops 294912 | bytes 3538944 | tf_op jit(solution)/shard_map/div | solution.py:481
Async XLA Ops:
  0.0 48.7 %copy-start = (f32[128,2304]{1,0:T(8,128)S(1)}, f32[128,2304]{1,0:T(8,128)}, u32[]{:S(2)}) copy-start(f32[128,2304]{1,0:T(8,128)} %param.8) | copy-start | bytes 3538948

commit v12 on v11

--- a/solution.py
+++ b/solution.py
@@ -280,16 +280,17 @@
         def _():
             fill_s(0)
 
-            @pl.when(jnp.logical_and(home == 1, ro == 1))
+            @pl.when(ro == 0)
             def _():
-                mirror()
-
-        @pl.when(jnp.logical_and(p == 2, ro == 0))
-        def _():
-            relay(0, s4)
-
-        @pl.when(jnp.logical_and(p == 2, ro == 1))
-        def _():
+                relay(0, s4)
+
+            @pl.when(jnp.logical_and(ro == 1, home == 0))
+            def _():
+                send(s4, smsg, s_copy, 1, 0, via)
+
+        @pl.when(jnp.logical_and(p == 2, jnp.logical_and(ro == 1, home == 1)))
+        def _():
+            mirror()
             send(s4, smsg, s_copy, 1, 0, via)
 
     d_d = tcopy(dg, whole, 5, _dev(c, o))

time: 50 us -> 49.3 us (0.986)
  Pallas kernels: 48.7 us -> 48 us
    pallas_call x1, Pallas kernels: 48.7 us -> 48 us  [sweep(): pl.pallas_call(sweep_kernel, out_shape=jax.ShapeDtypeStruct((n, w), F32),...]
where the time goes in v12:
time: 49.3 us; the launch traced here: 49.2 us
  Pallas kernels  48 us (97%)
  other arithmetic  1.17 us (2%)
    pallas_call x1, Pallas kernels, sweep(): pl.pallas_call(sweep_kernel, out_shape=jax.ShapeDtypeStruct((n, w), F32),...  48 us
    div x1, other arithmetic, local_sweep(): return sweep(t_blk, oovv_blk, vvvv_blk, oooo_full, wd_blk, wx_blk) / d_blk  1.17 us

profile of v12, /device:TPU:0, one launch (start us, length us, event | category | flops | bytes accessed | tf_op | source)
XLA Modules:
  0.0 49.2 jit_solution(10443258202727282010)
XLA Ops:
  0.0 0.0 copy-start
  0.0 48.0 %sweep.1 = f32[128,2304]{1,0:T(8,128)S(1)} custom-call(f32[128,2304]{1,0:T(8,128)} %t_hbm.1, bf16[128,2304]{1,0:T(8,128)(2,1)} %oovv_hbm.1, bf16[4608,2304]{1,0:T(8,128)(2,1)} %v_hbm.1, bf16[256,256]{1,0:T(8,128)(2,1)} %oooo_hbm.1, bf16[1536,384]{1,0:T(8,128)(2,1)} %wd_hbm.1, bf16[1536,384]{1,0:T(8,128)(2,1)} %wx_hbm.1), custom_call_target="tpu_custom_call" | custom-call | tf_op jit(solution)/shard_map/sweep/pallas_call | solution.py:458
  48.0 0.0 copy-done
  48.0 1.2 %div.3 = f32[128,2304]{1,0:T(8,128)} divide(f32[128,2304]{1,0:T(8,128)S(1)} %sweep.1, f32[128,2304]{1,0:T(8,128)S(1)} %copy-done) | non-fusion elementwise | flops 294912 | bytes 3538944 | tf_op jit(solution)/shard_map/div | solution.py:482
Async XLA Ops:
  0.0 48.0 %copy-start = (f32[128,2304]{1,0:T(8,128)S(1)}, f32[128,2304]{1,0:T(8,128)}, u32[]{:S(2)}) copy-start(f32[128,2304]{1,0:T(8,128)} %param.8) | copy-start | bytes 3538948

commit v13 on v12

--- a/solution.py
+++ b/solution.py
@@ -318,13 +318,25 @@
         mirror()
 
     send(s4, smsg, s_copy, 2, di, past)
-    send(s4, smsg, s_copy, 0, di, dg)
+
+    def across():
+        send(s4, smsg, s_copy, 0, di, dg)
+
+        @pl.when(home == 0)
+        def _():
+            send(st4, pmsg, p_copy, 0, di, dg)
 
     @pl.when(home == 0)
     def _():
         fill_t(di)
         send(st4, pmsg, p_copy, 2, di, past)
-        send(st4, pmsg, p_copy, 0, di, dg)
+
+    @pl.when(dg == 0)
+    def _():
+        across()
+
+    @pl.when(home == 0)
+    def _():
         send(st4, pmsg, p_copy, 3, ro, c)
         send(st4, pmsg, p_copy, 3, di, c)
 
@@ -387,6 +399,10 @@
         @pl.when(s == 5)
         def _():
             pass_on()
+
+        @pl.when(jnp.logical_and(s == 6, dg > 0))
+        def _():
+            across()
 
     landed(theirs, rrs).wait()
     landed(theirs, rs).wait()

time: 49.3 us -> 48.4 us (0.982)
  the two profiles are of different devices: /device:TPU:0 before, /device:TPU:1 now
where the time goes in v13:
time: 48.4 us; the launch traced here: 48.3 us
  Pallas kernels  47.1 us (97%)
  other arithmetic  1.17 us (2%)
    pallas_call x1, Pallas kernels, sweep(): pl.pallas_call(sweep_kernel, out_shape=jax.ShapeDtypeStruct((n, w), F32),...  47.1 us
    div x1, other arithmetic, local_sweep(): return sweep(t_blk, oovv_blk, vvvv_blk, oooo_full, wd_blk, wx_blk) / d_blk  1.17 us

profile of v13, /device:TPU:1, one launch (start us, length us, event | category | flops | bytes accessed | tf_op | source)
XLA Modules:
  0.0 48.3 jit_solution(9422305724460284076)
XLA Ops:
  0.0 0.0 copy-start
  0.0 47.1 %sweep.1 = f32[128,2304]{1,0:T(8,128)S(1)} custom-call(f32[128,2304]{1,0:T(8,128)} %t_hbm.1, bf16[128,2304]{1,0:T(8,128)(2,1)} %oovv_hbm.1, bf16[4608,2304]{1,0:T(8,128)(2,1)} %v_hbm.1, bf16[256,256]{1,0:T(8,128)(2,1)} %oooo_hbm.1, bf16[1536,384]{1,0:T(8,128)(2,1)} %wd_hbm.1, bf16[1536,384]{1,0:T(8,128)(2,1)} %wx_hbm.1), custom_call_target="tpu_custom_call" | custom-call | tf_op jit(solution)/shard_map/sweep/pallas_call | solution.py:474
  47.1 0.0 copy-done
  47.1 1.2 %div.3 = f32[128,2304]{1,0:T(8,128)} divide(f32[128,2304]{1,0:T(8,128)S(1)} %sweep.1, f32[128,2304]{1,0:T(8,128)S(1)} %copy-done) | non-fusion elementwise | flops 294912 | bytes 3538944 | tf_op jit(solution)/shard_map/div | solution.py:498
Async XLA Ops:
  0.0 47.1 %copy-start = (f32[128,2304]{1,0:T(8,128)S(1)}, f32[128,2304]{1,0:T(8,128)}, u32[]{:S(2)}) copy-start(f32[128,2304]{1,0:T(8,128)} %param.8) | copy-start | bytes 3538948

commit v14 on v13

--- a/solution.py
+++ b/solution.py
@@ -288,6 +288,10 @@
             def _():
                 send(s4, smsg, s_copy, 1, 0, via)
 
+        @pl.when(jnp.logical_and(p == 2, ro == 0))
+        def _():
+            send(s4, smsg, s_copy, 1, 0, via)
+
         @pl.when(jnp.logical_and(p == 2, jnp.logical_and(ro == 1, home == 1)))
         def _():
             mirror()
@@ -380,9 +384,9 @@
                          + jnp.dot(tg[2 * r + 1], vb[...], preferred_element_type=F32))
         ladder_copy(s).start()
 
-        @pl.when(s == 0)
-        def _():
-            send(s4, smsg, s_copy, 1, ro, via)
+        @pl.when(jnp.logical_and(s == 0, ro == 1))
+        def _():
+            send(s4, smsg, s_copy, 1, 1, via)
 
         @pl.when(jnp.logical_and(s == 1, di == 1))
         def _():

time: 48.4 us -> 48.5 us (level)
  no operation moved by 1% of the time
where the time goes in v14:
time: 48.5 us; the launch traced here: 48.4 us
  Pallas kernels  47.2 us (97%)
  other arithmetic  1.17 us (2%)
    pallas_call x1, Pallas kernels, sweep(): pl.pallas_call(sweep_kernel, out_shape=jax.ShapeDtypeStruct((n, w), F32),...  47.2 us
    div x1, other arithmetic, local_sweep(): return sweep(t_blk, oovv_blk, vvvv_blk, oooo_full, wd_blk, wx_blk) / d_blk  1.17 us

profile of v14, /device:TPU:1, one launch (start us, length us, event | category | flops | bytes accessed | tf_op | source)
XLA Modules:
  0.0 48.4 jit_solution(262053588246175389)
XLA Ops:
  0.0 0.0 copy-start
  0.0 47.2 %sweep.1 = f32[128,2304]{1,0:T(8,128)S(1)} custom-call(f32[128,2304]{1,0:T(8,128)} %t_hbm.1, bf16[128,2304]{1,0:T(8,128)(2,1)} %oovv_hbm.1, bf16[4608,2304]{1,0:T(8,128)(2,1)} %v_hbm.1, bf16[256,256]{1,0:T(8,128)(2,1)} %oooo_hbm.1, bf16[1536,384]{1,0:T(8,128)(2,1)} %wd_hbm.1, bf16[1536,384]{1,0:T(8,128)(2,1)} %wx_hbm.1), custom_call_target="tpu_custom_call" | custom-call | tf_op jit(solution)/shard_map/sweep/pallas_call | solution.py:478
  47.2 0.0 copy-done
  47.2 1.2 %div.3 = f32[128,2304]{1,0:T(8,128)} divide(f32[128,2304]{1,0:T(8,128)S(1)} %sweep.1, f32[128,2304]{1,0:T(8,128)S(1)} %copy-done) | non-fusion elementwise | flops 294912 | bytes 3538944 | tf_op jit(solution)/shard_map/div | solution.py:502
Async XLA Ops:
  0.0 47.2 %copy-start = (f32[128,2304]{1,0:T(8,128)S(1)}, f32[128,2304]{1,0:T(8,128)}, u32[]{:S(2)}) copy-start(f32[128,2304]{1,0:T(8,128)} %param.8) | copy-start | bytes 3538948

commit v15 on v13

--- a/solution.py
+++ b/solution.py
@@ -396,11 +396,11 @@
         def _():
             send(st4, pmsg, p_copy, 1, di, via)
 
-        @pl.when(s == 5)
+        @pl.when(s == 4)
         def _():
             pass_on()
 
-        @pl.when(jnp.logical_and(s == 6, dg > 0))
+        @pl.when(jnp.logical_and(s == 7, dg > 0))
         def _():
             across()
 

time: 48.4 us -> 48.4 us (level)
  no operation moved by 1% of the time
where the time goes in v15:
time: 48.4 us; the launch traced here: 48.3 us
  Pallas kernels  47.1 us (97%)
  other arithmetic  1.17 us (2%)
    pallas_call x1, Pallas kernels, sweep(): pl.pallas_call(sweep_kernel, out_shape=jax.ShapeDtypeStruct((n, w), F32),...  47.1 us
    div x1, other arithmetic, local_sweep(): return sweep(t_blk, oovv_blk, vvvv_blk, oooo_full, wd_blk, wx_blk) / d_blk  1.17 us

profile of v15, /device:TPU:1, one launch (start us, length us, event | category | flops | bytes accessed | tf_op | source)
XLA Modules:
  0.0 48.3 jit_solution(15279703648053991457)
XLA Ops:
  0.0 0.0 copy-start
  0.0 47.1 %sweep.1 = f32[128,2304]{1,0:T(8,128)S(1)} custom-call(f32[128,2304]{1,0:T(8,128)} %t_hbm.1, bf16[128,2304]{1,0:T(8,128)(2,1)} %oovv_hbm.1, bf16[4608,2304]{1,0:T(8,128)(2,1)} %v_hbm.1, bf16[256,256]{1,0:T(8,128)(2,1)} %oooo_hbm.1, bf16[1536,384]{1,0:T(8,128)(2,1)} %wd_hbm.1, bf16[1536,384]{1,0:T(8,128)(2,1)} %wx_hbm.1), custom_call_target="tpu_custom_call" | custom-call | tf_op jit(solution)/shard_map/sweep/pallas_call | solution.py:474
  47.1 0.0 copy-done
  47.1 1.2 %div.3 = f32[128,2304]{1,0:T(8,128)} divide(f32[128,2304]{1,0:T(8,128)S(1)} %sweep.1, f32[128,2304]{1,0:T(8,128)S(1)} %copy-done) | non-fusion elementwise | flops 294912 | bytes 3538944 | tf_op jit(solution)/shard_map/div | solution.py:498
Async XLA Ops:
  0.0 47.1 %copy-start = (f32[128,2304]{1,0:T(8,128)S(1)}, f32[128,2304]{1,0:T(8,128)}, u32[]{:S(2)}) copy-start(f32[128,2304]{1,0:T(8,128)} %param.8) | copy-start | bytes 3538948

commit v16 on v13

--- a/solution.py
+++ b/solution.py
@@ -317,8 +317,6 @@
     def _():
         mirror()
 
-    send(s4, smsg, s_copy, 2, di, past)
-
     def across():
         send(s4, smsg, s_copy, 0, di, dg)
 
@@ -329,11 +327,16 @@
     @pl.when(home == 0)
     def _():
         fill_t(di)
+
+    @pl.when(dg == 0)
+    def _():
+        across()
+
+    send(s4, smsg, s_copy, 2, di, past)
+
+    @pl.when(home == 0)
+    def _():
         send(st4, pmsg, p_copy, 2, di, past)
-
-    @pl.when(dg == 0)
-    def _():
-        across()
 
     @pl.when(home == 0)
     def _():

time: 48.4 us -> 48.3 us (level)
  no operation moved by 1% of the time
where the time goes in v16:
time: 48.3 us; the launch traced here: 48.2 us
  Pallas kernels  47 us (97%)
  other arithmetic  1.17 us (2%)
    pallas_call x1, Pallas kernels, sweep(): pl.pallas_call(sweep_kernel, out_shape=jax.ShapeDtypeStruct((n, w), F32),...  47 us
    div x1, other arithmetic, local_sweep(): return sweep(t_blk, oovv_blk, vvvv_blk, oooo_full, wd_blk, wx_blk) / d_blk  1.17 us

profile of v16, /device:TPU:1, one launch (start us, length us, event | category | flops | bytes accessed | tf_op | source)
XLA Modules:
  0.0 48.2 jit_solution(7239367412489598088)
XLA Ops:
  0.0 0.0 copy-start
  0.0 47.0 %sweep.1 = f32[128,2304]{1,0:T(8,128)S(1)} custom-call(f32[128,2304]{1,0:T(8,128)} %t_hbm.1, bf16[128,2304]{1,0:T(8,128)(2,1)} %oovv_hbm.1, bf16[4608,2304]{1,0:T(8,128)(2,1)} %v_hbm.1, bf16[256,256]{1,0:T(8,128)(2,1)} %oooo_hbm.1, bf16[1536,384]{1,0:T(8,128)(2,1)} %wd_hbm.1, bf16[1536,384]{1,0:T(8,128)(2,1)} %wx_hbm.1), custom_call_target="tpu_custom_call" | custom-call | tf_op jit(solution)/shard_map/sweep/pallas_call | solution.py:477
  47.0 0.0 copy-done
  47.0 1.2 %div.3 = f32[128,2304]{1,0:T(8,128)} divide(f32[128,2304]{1,0:T(8,128)S(1)} %sweep.1, f32[128,2304]{1,0:T(8,128)S(1)} %copy-done) | non-fusion elementwise | flops 294912 | bytes 3538944 | tf_op jit(solution)/shard_map/div | solution.py:501
Async XLA Ops:
  0.0 47.0 %copy-start = (f32[128,2304]{1,0:T(8,128)S(1)}, f32[128,2304]{1,0:T(8,128)}, u32[]{:S(2)}) copy-start(f32[128,2304]{1,0:T(8,128)} %param.8) | copy-start | bytes 3538948
